TPU v7x, 32 devices: a whole 2x2x4 slice. The times are simulated.
32 devices in a mesh: atom: 4 (over y, x), tm: 8 (over z, core).
Axes of the slice: x: 2, y: 2, z: 4, core: 2. Of those that a mesh axis runs over, the one named last changes fastest.
Arguments:
- signal: bfloat16 [306, 8192], P(None, 'tm'), may hold values from -6 to 6
- spatial: bfloat16 [256, 306], P('atom'), may hold values from -0.3125 to 0.3125
- temporal: bfloat16 [256, 256], P('atom'), may hold values from -0.375 to 0.375
- code_values: bfloat16 [256, 8192], P('atom', 'tm'), may hold values from 0 to 2
- block_mask: int32 [256, 32], P('atom', 'tm'), may hold values 0 or 1
Outputs:
- grad_spatial: float32 [256, 306], P('atom')
- grad_temporal: float32 [256, 256], P('atom')
All inputs are finite; a program needn't handle non-finite values. No bound on the sum of `block_mask` on one device may be relied on, other than what follows from the above.
Results may differ from a plain program's by a relative error of at most 0.0025.
Values may be sent and summed in bfloat16 or wider, within the bound.
A program may use at most 64 MiB of HBM per device.

v0:
```python
import functools
import math

import jax
import jax.numpy as jnp
from jax import lax
from jax.experimental import pallas as pl
from jax.experimental.pallas import tpu as pltpu
from jax.sharding import PartitionSpec as P

LANES = 128
ROWS = 128
MESH = pl.DeviceIdType.MESH
F32 = jnp.float32
BF16 = jnp.bfloat16


def kernel(
    n_atom, n_tm, factor,
    signal_ref, spatial_ref, temporal_ref, values_ref, mask_ref,
    out_sp_ref, out_tm_ref,
    tail, halo, x, w, cbuf, ctbuf, sbuf, weights, own_w, sig, sig_t, proj, sums, taps,
    sp_part, sp_recv, sp_full, tm_part, tm_recv, tm_full,
    halo_sems, s_send, s_recv, c_send, c_recv,
    sp_send, sp_rsem, sp_gsend, sp_grecv, tm_send, tm_rsem, tm_gsend, tm_grecv,
):
    atoms, channels = spatial_ref.shape
    length = temporal_ref.shape[1]
    samples = signal_ref.shape[1]
    blocks = mask_ref.shape[0]
    block = samples // blocks
    fold = LANES // atoms
    seg = samples // fold
    chunks = seg // ROWS
    share = atoms // n_tm
    me_a = lax.axis_index("atom")
    me_t = lax.axis_index("tm")
    a_peers = [lax.rem(me_a + d, n_atom) for d in range(1, n_atom)]
    t_peers = [lax.rem(me_t + d, n_tm) for d in range(1, n_tm)]

    barrier = pltpu.get_barrier_semaphore()
    for peer in a_peers:
        pl.semaphore_signal(barrier, inc=1, device_id={"atom": peer}, device_id_type=MESH)
    for peer in t_peers:
        pl.semaphore_signal(barrier, inc=1, device_id={"tm": peer}, device_id_type=MESH)

    mask = mask_ref[...].astype(F32).T
    codes = jnp.concatenate(
        [
            values_ref[:, j * block : (j + 1) * block].astype(F32) * mask[:, j : j + 1]
            for j in range(blocks)
        ],
        axis=1,
    )
    tail[...] = codes[:, samples - length :].astype(BF16)

    def enter():

        right = lax.rem(me_t + 1, n_tm)
        halo_copy = pltpu.make_async_remote_copy(
            src_ref=tail, dst_ref=halo, send_sem=halo_sems.at[0], recv_sem=halo_sems.at[1],
            device_id={"tm": right}, device_id_type=MESH,
        )

        @pl.when(me_t < n_tm - 1)
        def _():
            halo_copy.start()

        s_copies = []
        for d, peer in enumerate(a_peers):
            copy = pltpu.make_async_remote_copy(
                src_ref=spatial_ref, dst_ref=sbuf.at[me_a], send_sem=s_send.at[d],
                recv_sem=s_recv.at[d], device_id={"atom": peer}, device_id_type=MESH,
            )
            copy.start()
            s_copies.append(copy)
        return halo_copy, s_copies

    stacked = jnp.concatenate([codes[:, h * seg : (h + 1) * seg] for h in range(fold)], axis=0)
    x[length:, :] = stacked.T
    w[...] = jnp.concatenate([temporal_ref[...].astype(F32)] * fold, axis=0).T

    c_copies = [[None] * (n_atom - 1) for _ in range(chunks)]

    def convolve(c):
        base = length + c * ROWS

        def body(a, acc):
            for b in range(8):
                start = pl.multiple_of(base - 24 - 32 * a, 8) - b
                xs = x[pl.ds(start, ROWS + 24), :]
                for q in range(4):
                    tap = w[pl.ds(32 * a + 8 * q + b, 1), :]
                    acc = acc + xs[24 - 8 * q : 24 - 8 * q + ROWS] * tap
            return acc

        acc = lax.fori_loop(0, length // 32, body, jnp.zeros((ROWS, LANES), F32))
        course = acc.astype(BF16)
        rows = pl.ds(c * ROWS, ROWS)
        cbuf[me_a, rows, :] = course
        ctbuf[c] = course.astype(F32).T.astype(BF16)

    def send(c):
        rows = pl.ds(c * ROWS, ROWS)
        for d, peer in enumerate(a_peers):
            copy = pltpu.make_async_remote_copy(
                src_ref=cbuf.at[me_a, rows], dst_ref=cbuf.at[me_a, rows],
                send_sem=c_send.at[d, c], recv_sem=c_recv.at[d, c],
                device_id={"atom": peer}, device_id_type=MESH,
            )
            copy.start()
            c_copies[c][d] = copy

    late = [c for c in range(chunks) if c * ROWS >= length]
    early = [c for c in range(chunks) if c * ROWS < length]
    if not late:
        pl.semaphore_wait(barrier, n_atom - 1 + n_tm - 1)
        halo_copy, s_copies = enter()
    for i, c in enumerate(late):
        convolve(c)
        if i == 0:
            pl.semaphore_wait(barrier, n_atom - 1 + n_tm - 1)
            halo_copy, s_copies = enter()
        send(c)

    padded = sig.shape[0]
    sig[channels // 8 * 8 :, :] = jnp.zeros((padded - channels // 8 * 8, samples), F32)
    sig[:channels, :] = signal_ref[...].astype(F32)
    for c in range(samples // ROWS):
        sig_t[c * ROWS : (c + 1) * ROWS, :] = sig[:, c * ROWS : (c + 1) * ROWS].T

    @pl.when(me_t == 0)
    def _():
        halo[...] = jnp.zeros(halo.shape, halo.dtype)

    @pl.when(me_t > 0)
    def _():
        halo_copy.wait_recv()

    before = jnp.concatenate(
        [halo[...].astype(F32)] + [codes[:, h * seg - length : h * seg] for h in range(1, fold)],
        axis=0,
    )
    x[:length, :] = before.T
    for c in early:
        convolve(c)
        send(c)

    sbuf[me_a] = spatial_ref[...]
    for copy in s_copies:
        copy.wait_recv()
    weights[...] = jnp.zeros(weights.shape, BF16)
    own_w[...] = jnp.zeros(own_w.shape, BF16)
    for h in range(fold):
        for g in range(n_atom):
            weights[h, g * LANES + h * atoms : g * LANES + (h + 1) * atoms, :channels] = sbuf[g]
        own_w[h, h * atoms : (h + 1) * atoms, :channels] = spatial_ref[...]

    def process(c, gsp):
        for copy in c_copies[c]:
            copy.wait_recv()
        rows = slice(c * ROWS, (c + 1) * ROWS)
        lhs = jnp.concatenate([cbuf[g, rows, :] for g in range(n_atom)], axis=1)
        projected = None
        for h in range(fold):
            model = jnp.dot(lhs, weights[h], preferred_element_type=F32)
            at = h * seg + c * ROWS
            residual = (model - sig_t[at : at + ROWS, :]).astype(BF16)
            part = lax.dot_general(
                residual, own_w[h], (((1,), (1,)), ((), ())), preferred_element_type=F32
            )
            projected = part if projected is None else projected + part
            grad = jnp.dot(
                ctbuf[c, h * atoms : (h + 1) * atoms, :], residual, preferred_element_type=F32
            )
            gsp = grad if gsp is None else gsp + grad
        proj[rows, :] = projected.astype(BF16).astype(F32)
        return gsp

    def scatter(part, recv, send_sems, recv_sems):
        copies = []
        for d, peer in enumerate(t_peers):
            copy = pltpu.make_async_remote_copy(
                src_ref=part.at[peer], dst_ref=recv.at[d], send_sem=send_sems.at[d],
                recv_sem=recv_sems.at[d], device_id={"tm": peer}, device_id_type=MESH,
            )
            copy.start()
            copies.append(copy)
        return copies

    def gather(part, recv, full, copies, send_sems, recv_sems):
        total = part[me_t]
        for d, copy in enumerate(copies):
            copy.wait_recv()
            total = total + recv[d]
        full[me_t] = total * factor
        sent = []
        for d, peer in enumerate(t_peers):
            copy = pltpu.make_async_remote_copy(
                src_ref=full.at[me_t], dst_ref=full.at[me_t], send_sem=send_sems.at[d],
                recv_sem=recv_sems.at[d], device_id={"tm": peer}, device_id_type=MESH,
            )
            copy.start()
            sent.append(copy)
        return sent

    def correlate(c, lo, hi, first, last):
        def body(a, carry):
            p = proj[c * ROWS : (c + 1) * ROWS, :]
            for b in range(8):
                start = pl.multiple_of(length + c * ROWS - 56 - 64 * a, 8) - b
                xs = x[pl.ds(start, ROWS + 56), :]
                for q in range(8):
                    slot = pl.ds(pl.multiple_of(((a * 8 + b) * 8 + q) * 8, 8), 8)
                    acc = None if first else sums[slot, :]
                    piece = p * xs[56 - 8 * q : 56 - 8 * q + ROWS]
                    for i in range(ROWS // 8):
                        row = piece[8 * i : 8 * i + 8]
                        acc = row if acc is None else acc + row
                    if last:
                        tau = pl.ds(64 * a + 8 * q + b, 1)
                        taps[tau, :] = jnp.sum(acc, axis=0, keepdims=True)
                    else:
                        sums[slot, :] = acc
            return carry

        lax.fori_loop(lo, hi, body, 0)

    halves = tm_part.shape[0]
    width = length // halves
    steps = length // 64
    order = late + early
    near = order[: chunks // 2]
    gsp = None
    for c in near:
        gsp = process(c, gsp)
        correlate(c, 0, steps, c == order[0], False)
    for c in order[chunks // 2 :]:
        gsp = process(c, gsp)
    for j in range(n_tm):
        sp_part[j] = gsp[j * share : (j + 1) * share, :]
    sp_copies = scatter(sp_part, sp_recv, sp_send, sp_rsem)
    for c in order[chunks // 2 : -1]:
        correlate(c, 0, steps, c == order[0], False)
    tm_copies = []
    for half in range(halves):
        correlate(order[-1], half * width // 64, (half + 1) * width // 64, False, True)
        spread = taps[half * width : (half + 1) * width, :].T
        gtm = spread[:atoms]
        for h in range(1, fold):
            gtm = gtm + spread[h * atoms : (h + 1) * atoms]
        for j in range(n_tm):
            tm_part[half, j] = gtm[j * share : (j + 1) * share, :]
        tm_copies.append(
            scatter(tm_part.at[half], tm_recv.at[half], tm_send.at[half], tm_rsem.at[half])
        )
        if half == 0:
            sp_sent = gather(sp_part, sp_recv, sp_full, sp_copies, sp_gsend, sp_grecv)
    tm_sent = []
    for half in range(halves):
        tm_sent.append(
            gather(
                tm_part.at[half], tm_recv.at[half], tm_full.at[half], tm_copies[half],
                tm_gsend.at[half], tm_grecv.at[half],
            )
        )

    for copy in sp_sent:
        copy.wait_recv()
    for j in range(n_tm):
        out_sp_ref[j * share : (j + 1) * share, :] = sp_full[j][:, :channels]
    for half in range(halves):
        for copy in tm_sent[half]:
            copy.wait_recv()
        for j in range(n_tm):
            out_tm_ref[j * share : (j + 1) * share, half * width : (half + 1) * width] = tm_full[half, j]

    @pl.when(me_t < n_tm - 1)
    def _():
        halo_copy.wait_send()

    for copy in s_copies + [copy for row in c_copies for copy in row]:
        copy.wait_send()
    for copy in sp_copies + sp_sent:
        copy.wait_send()
    for row in tm_copies + tm_sent:
        for copy in row:
            copy.wait_send()


def local(n_atom, n_tm, signal, spatial, temporal, values, mask):
    atoms, channels = spatial.shape
    length = temporal.shape[1]
    samples = signal.shape[1]
    fold = LANES // atoms
    seg = samples // fold
    chunks = seg // ROWS
    share = atoms // n_tm
    wide = -(-channels // LANES) * LANES
    halves = 1
    width = length // halves
    factor = 1.0 / math.sqrt(samples * n_tm)
    dma = pltpu.SemaphoreType.DMA
    vmem = pl.BlockSpec(memory_space=pltpu.VMEM)
    return pl.pallas_call(
        functools.partial(kernel, n_atom, n_tm, factor),
        out_shape=(
            pltpu.VMEM((atoms, channels), F32),
            pltpu.VMEM((atoms, length), F32),
        ),
        in_specs=[vmem] * 5,
        out_specs=(vmem, vmem),
        scratch_shapes=[
            pltpu.VMEM((atoms, length), BF16),
            pltpu.VMEM((atoms, length), BF16),
            pltpu.VMEM((length + seg, LANES), F32),
            pltpu.VMEM((length, LANES), F32),
            pltpu.VMEM((n_atom, seg, LANES), BF16),
            pltpu.VMEM((chunks, LANES, ROWS), BF16),
            pltpu.VMEM((n_atom, atoms, channels), BF16),
            pltpu.VMEM((fold, n_atom * LANES, wide), BF16),
            pltpu.VMEM((fold, LANES, wide), BF16),
            pltpu.VMEM((wide, samples), F32),
            pltpu.VMEM((samples, wide), F32),
            pltpu.VMEM((seg, LANES), F32),
            pltpu.VMEM((8 * length, LANES), F32),
            pltpu.VMEM((length, LANES), F32),
            pltpu.VMEM((n_tm, share, wide), F32),
            pltpu.VMEM((n_tm - 1, share, wide), F32),
            pltpu.VMEM((n_tm, share, wide), F32),
            pltpu.VMEM((halves, n_tm, share, width), F32),
            pltpu.VMEM((halves, n_tm - 1, share, width), F32),
            pltpu.VMEM((halves, n_tm, share, width), F32),
            dma((2,)),
            dma((n_atom - 1,)),
            dma((n_atom - 1,)),
            dma((n_atom - 1, chunks)),
            dma((n_atom - 1, chunks)),
            dma((n_tm - 1,)),
            dma((n_tm - 1,)),
            dma((n_tm - 1,)),
            dma((n_tm - 1,)),
            dma((halves, n_tm - 1)),
            dma((halves, n_tm - 1)),
            dma((halves, n_tm - 1)),
            dma((halves, n_tm - 1)),
        ],
        compiler_params=pltpu.CompilerParams(collective_id=0, has_side_effects=True),
    )(signal, spatial, temporal, values, mask.T)


def solution(mesh):
    in_specs = (P(None, "tm"), P("atom", None), P("atom", None), P("atom", "tm"), P("atom", "tm"))
    out_specs = (P("atom", None), P("atom", None))
    body = functools.partial(local, mesh.shape["atom"], mesh.shape["tm"])
    return jax.shard_map(body, mesh=mesh, in_specs=in_specs, out_specs=out_specs, check_vma=False)
```

profile of v0, /device:TPU:0, one launch (start us, length us, event | category | flops | bytes accessed | tf_op | source)
XLA Modules:
  0.0 31.2 jit_solution(2961085919750777347)
XLA Ops:
  0.6 29.3 %shard_map.68 = (f32[64,306]{1,0:T(8,128)S(1)}, f32[64,256]{1,0:T(8,128)S(1)}) custom-call(bf16[306,1024]{1,0:T(8,128)(2,1)} %signal_ref.1, bf16[64,306]{1,0:T(8,128)(2,1)} %spatial_ref.1, bf16[64,256]{1,0:T(8,128)(2,1)} %temporal_ref.1, bf16[64,1024]{1,0:T(8,128)(2,1)} %values_ref.1, s32[4,64]{1,0:T(4,128)} %bitcast.1), custom_call_target="tpu_custom_call" | custom-call | tf_op jit(solution)/shard_map/pallas_call | solution.py:305
  29.9 0.6 %copy.9 = f32[64,306]{1,0:T(8,128)} copy(f32[64,306]{1,0:T(8,128)S(1)} %get-tuple-element.2) | data formatting | bytes 156672
  30.5 0.6 %copy.10 = f32[64,256]{1,0:T(8,128)} copy(f32[64,256]{1,0:T(8,128)S(1)} %get-tuple-element.3) | data formatting | bytes 131072
where the time goes:
time: 31.3 us; the launch traced here: 31.2 us
  Pallas kernels  29.3 us (94%)
  local copies, waits for them, and re-layouts  1.27 us (4%)
  between operations  0.64 us (2%)
    pallas_call x1, Pallas kernels, local(): pl.pallas_call(functools.partial(kernel, n_atom, n_tm, factor), out_shape...  29.3 us
    unnamed x2, local copies, waits for them, and re-layouts  1.27 us

commit v1 on v0

v1 whole, which is shorter than its diff:
```python
import functools
import math

import jax
import jax.numpy as jnp
from jax import lax
from jax.experimental import pallas as pl
from jax.experimental.pallas import tpu as pltpu
from jax.sharding import PartitionSpec as P

W = 128
B = 32
GROUP = 16
MESH = pl.DeviceIdType.MESH
F32 = jnp.float32
BF16 = jnp.bfloat16


def kernel(
    n_atom, n_tm, factor,
    signal_ref, spatial_ref, temporal_ref, values_ref, mask_ref,
    out_sp_ref, out_tm_ref,
    tail, halo, cx, xt, wt, tbuf, cf, cbuf, sbuf, sp32, st, own_w, resb, pj, lt, gt,
    part, recv1, half, total,
    halo_sems, s_send, s_recv, c_send, c_recv,
    p_send, p_recv, z_send, z_recv, f_send, f_recv,
):
    atoms, channels = spatial_ref.shape
    length = temporal_ref.shape[1]
    samples = signal_ref.shape[1]
    blocks = mask_ref.shape[0]
    block = samples // blocks
    nb = samples // W
    hb = length // W
    chunk = length
    chunks = samples // chunk
    per = chunk // W
    rows_p = st.shape[0]
    wide = sp32.shape[1]
    chips = n_tm // 2
    me_a = lax.axis_index("atom")
    me_t = lax.axis_index("tm")
    me_z = me_t // 2
    core = lax.rem(me_t, 2)
    partner = me_z * 2 + 1 - core
    a_peers = [lax.rem(me_a + d, n_atom) for d in range(1, n_atom)]
    t_peers = [lax.rem(me_t + d, n_tm) for d in range(1, n_tm)]
    z_peers = [lax.rem(me_z + d, chips) for d in range(1, chips)]
    mine = pl.ds(pl.multiple_of(me_a * atoms, atoms), atoms)

    barrier = pltpu.get_barrier_semaphore()
    for peer in a_peers:
        pl.semaphore_signal(barrier, inc=1, device_id={"atom": peer}, device_id_type=MESH)
    for peer in t_peers:
        pl.semaphore_signal(barrier, inc=1, device_id={"tm": peer}, device_id_type=MESH)

    mask = mask_ref[...].astype(F32).T
    codes = [
        values_ref[:, j * block : (j + 1) * block].astype(F32) * mask[:, j : j + 1]
        for j in range(blocks)
    ]
    codes = jnp.concatenate(codes, axis=1)
    tail[...] = codes[:, samples - length :].astype(BF16)
    cx[: hb * atoms, :] = jnp.zeros((hb * atoms, W), F32)
    for b in range(nb):
        cx[(hb + b) * atoms : (hb + b + 1) * atoms, :] = codes[:, b * W : (b + 1) * W]
    for d in range(hb):
        wt[d * atoms : (d + 1) * atoms, :] = temporal_ref[:, d * W : (d + 1) * W].astype(F32)

    row = lax.broadcasted_iota(jnp.int32, (W, W), 0)
    col = lax.broadcasted_iota(jnp.int32, (W, W), 1)
    ahead = col >= row

    def toeplitz(k):
        circ = [
            pltpu.roll(
                jnp.broadcast_to(wt[pl.ds(d * atoms + k, 1), :], (W, W)),
                0, 1, stride=1, stride_axis=0,
            )
            for d in range(hb)
        ]
        zero = jnp.zeros((W, W), F32)
        parts = []
        for d in range(hb, -1, -1):
            near = circ[d] if d < hb else zero
            far = circ[d - 1] if d > 0 else zero
            parts.append(jnp.where(ahead, near, far))
        return jnp.concatenate(parts, axis=0)

    def windows(k):
        return jnp.concatenate(
            [cx[pl.ds(j * atoms + k, nb, stride=atoms), :] for j in range(hb + 1)], axis=1
        )

    def apply(p, taps):
        k = 2 * p
        lhs = jnp.concatenate([windows(k), windows(k + 1)], axis=0).astype(BF16)
        out = jnp.dot(lhs, taps, preferred_element_type=F32)
        cf[pl.ds(k, nb, stride=atoms), :] = out[:nb, :W]
        cf[pl.ds(k + 1, nb, stride=atoms), :] = out[nb:, W:]

    def first(p, carry):
        k = 2 * p
        taps = jnp.concatenate([toeplitz(k), toeplitz(k + 1)], axis=1).astype(BF16)
        tbuf[p] = taps
        apply(p, taps)
        return carry

    def again(p, carry):
        apply(p, tbuf[p])
        return carry

    lax.fori_loop(0, atoms // 2, first, 0)

    pl.semaphore_wait(barrier, n_atom - 1 + n_tm - 1)

    right = lax.rem(me_t + 1, n_tm)
    halo_copy = pltpu.make_async_remote_copy(
        src_ref=tail, dst_ref=halo, send_sem=halo_sems.at[0], recv_sem=halo_sems.at[1],
        device_id={"tm": right}, device_id_type=MESH,
    )

    @pl.when(me_t < n_tm - 1)
    def _():
        halo_copy.start()

    c_copies = [[None] * (n_atom - 1) for _ in range(chunks)]

    def send(c):
        for b in range(per):
            at = c * per + b
            cbuf[c, mine, b * W : (b + 1) * W] = cf[at * atoms : (at + 1) * atoms, :].astype(BF16)
        for d, peer in enumerate(a_peers):
            copy = pltpu.make_async_remote_copy(
                src_ref=cbuf.at[c, mine], dst_ref=cbuf.at[c, mine],
                send_sem=c_send.at[d, c], recv_sem=c_recv.at[d, c],
                device_id={"atom": peer}, device_id_type=MESH,
            )
            copy.start()
            c_copies[c][d] = copy

    s_copies = []
    for d, peer in enumerate(a_peers):
        copy = pltpu.make_async_remote_copy(
            src_ref=spatial_ref, dst_ref=sbuf.at[mine], send_sem=s_send.at[d],
            recv_sem=s_recv.at[d], device_id={"atom": peer}, device_id_type=MESH,
        )
        copy.start()
        s_copies.append(copy)
    for c in range(1, chunks):
        send(c)

    xt[length : length + samples, :atoms] = codes.T
    xt[length + samples :, :] = jnp.zeros((xt.shape[0] - length - samples, W), F32)
    pj[...] = jnp.zeros(pj.shape, F32)
    resb[:, channels // 16 * 16 :, :] = jnp.zeros(
        (chunks, rows_p - channels // 16 * 16, chunk), BF16
    )
    sp32[...] = jnp.zeros(sp32.shape, F32)

    @pl.when(me_t == 0)
    def _():
        halo[...] = jnp.zeros(halo.shape, halo.dtype)

    @pl.when(me_t > 0)
    def _():
        halo_copy.wait_recv()

    before = halo[...].astype(F32)
    for b in range(hb):
        cx[b * atoms : (b + 1) * atoms, :] = before[:, b * W : (b + 1) * W]
    lax.fori_loop(0, atoms // 2, again, 0)
    send(0)
    xt[:length, :atoms] = before.T

    per_block = W // B

    def lay(i, carry):
        s = B - 1 - i
        picked = jnp.concatenate(
            [xt[pl.ds(B * r + s, GROUP, stride=W), :] for r in range(per_block)], axis=0
        )
        lt[pl.ds(pl.multiple_of(i * atoms, atoms), atoms), : per_block * GROUP] = picked.T[:atoms]
        return carry

    lax.fori_loop(0, B, lay, 0)

    sbuf[mine, :] = spatial_ref[...]
    for copy in s_copies:
        copy.wait_recv()
    sp32[:, :channels] = sbuf[...].astype(F32)
    st[...] = sp32[...].T[:rows_p].astype(BF16)
    own_w[...] = sp32[mine, :rows_p].astype(BF16)

    def process(c, gsp):
        for copy in c_copies[c]:
            copy.wait_recv()
        model = jnp.dot(st[...], cbuf[c], preferred_element_type=F32)
        resb[c, :channels, :] = (
            model[:channels] - signal_ref[:, c * chunk : (c + 1) * chunk].astype(F32)
        ).astype(BF16)
        residual = resb[c]
        projected = jnp.dot(own_w[...], residual, preferred_element_type=F32)
        projected = projected.astype(BF16).astype(F32)
        for b in range(per):
            at = hb + c * per + b
            pj[0, at * atoms : (at + 1) * atoms, :] = projected[:, b * W : (b + 1) * W]
        grad = lax.dot_general(
            cbuf[c, mine, :], residual, (((1,), (1,)), ((), ())), preferred_element_type=F32
        )
        return grad if gsp is None else gsp + grad

    gsp = None
    for c in list(range(1, chunks)) + [0]:
        gsp = process(c, gsp)

    low = pl.ds(pl.multiple_of(core * (atoms // 2), atoms // 2), atoms // 2)
    other = pl.ds(pl.multiple_of((1 - core) * (atoms // 2), atoms // 2), atoms // 2)

    def swap(i, lanes):
        copy = pltpu.make_async_remote_copy(
            src_ref=part.at[i, other, lanes], dst_ref=recv1.at[i, :, lanes],
            send_sem=p_send.at[i], recv_sem=p_recv.at[i],
            device_id={"tm": partner}, device_id_type=MESH,
        )
        copy.start()
        return copy

    def spread(i, lanes, copy):
        copy.wait_recv()
        half[i, me_z, :, lanes] = part[i, low, lanes] + recv1[i, :, lanes]
        copies = []
        for d, peer in enumerate(z_peers):
            out = pltpu.make_async_remote_copy(
                src_ref=half.at[i, me_z, :, lanes], dst_ref=half.at[i, me_z, :, lanes],
                send_sem=z_send.at[i, d], recv_sem=z_recv.at[i, d],
                device_id={"tm": peer * 2 + core}, device_id_type=MESH,
            )
            out.start()
            copies.append(out)
        return copies

    def finish(i, lanes, copies):
        for copy in copies:
            copy.wait_recv()
        acc = half[i, 0, :, lanes]
        for z in range(1, chips):
            acc = acc + half[i, z, :, lanes]
        total[i, low, lanes] = acc * factor
        copy = pltpu.make_async_remote_copy(
            src_ref=total.at[i, low, lanes], dst_ref=total.at[i, low, lanes],
            send_sem=f_send.at[i], recv_sem=f_recv.at[i],
            device_id={"tm": partner}, device_id_type=MESH,
        )
        copy.start()
        return copy

    sp_lanes = slice(0, wide)
    tm_lanes = slice(0, length)
    part[0, :, :rows_p] = gsp
    if rows_p < wide:
        part[0, :, rows_p:] = jnp.zeros((atoms, wide - rows_p), F32)
    swap_sp = swap(0, sp_lanes)

    lane = lax.broadcasted_iota(jnp.int32, (atoms, W), 1)
    for r in range(1, per_block):
        turned = [
            pltpu.roll(pj[0, i * atoms : (i + 1) * atoms, :], W - B * r, 1)
            for i in range(hb, hb + nb)
        ]
        turned = [jnp.zeros((atoms, W), F32)] + turned + [jnp.zeros((atoms, W), F32)]
        for n in range(nb + 1):
            i = hb - 1 + n
            pj[r, i * atoms : (i + 1) * atoms, :] = jnp.where(
                lane < W - B * r, turned[n], turned[n + 1]
            )

    spread_sp = spread(0, sp_lanes, swap_sp)

    depth = (length + B - 1) // W + 1

    def correlate(k, carry):
        lhs = lt[pl.ds(k, B, stride=atoms), :][:, : per_block * GROUP].astype(BF16)
        rhs = jnp.concatenate(
            [
                jnp.concatenate(
                    [pj[r, pl.ds(j * atoms + k, GROUP, stride=atoms), :] for r in range(per_block)],
                    axis=0,
                )
                for j in range(depth)
            ],
            axis=1,
        ).astype(BF16)
        prod = jnp.dot(lhs, rhs, preferred_element_type=F32)
        prod = pltpu.roll(prod, depth * W - (B - 1), 1, stride=1, stride_axis=0)[:, :length]
        acc = prod[:8]
        for i in range(1, B // 8):
            acc = acc + prod[8 * i : 8 * i + 8]
        for d in range(hb):
            gt[pl.ds(pl.multiple_of(8 * (d * atoms + k), 8), 8), :] = acc[:, d * W : (d + 1) * W]
        return carry

    lax.fori_loop(0, atoms, correlate, 0)
    for d in range(hb):
        gtm = gt[pl.ds(8 * d * atoms, atoms, stride=8), :]
        for i in range(1, 8):
            gtm = gtm + gt[pl.ds(8 * d * atoms + i, atoms, stride=8), :]
        part[1, :, d * W : (d + 1) * W] = gtm
    swap_tm = swap(1, tm_lanes)
    spread_tm = spread(1, tm_lanes, swap_tm)
    last_sp = finish(0, sp_lanes, spread_sp)
    last_tm = finish(1, tm_lanes, spread_tm)
    last_sp.wait_recv()
    out_sp_ref[...] = total[0, :, :channels]
    last_tm.wait_recv()
    out_tm_ref[...] = total[1, :, :length]

    @pl.when(me_t < n_tm - 1)
    def _():
        halo_copy.wait_send()

    for copy in s_copies + [copy for line in c_copies for copy in line]:
        copy.wait_send()
    for copy in [swap_sp, swap_tm, last_sp, last_tm] + spread_sp + spread_tm:
        copy.wait_send()


def local(n_atom, n_tm, signal, spatial, temporal, values, mask):
    atoms, channels = spatial.shape
    length = temporal.shape[1]
    samples = signal.shape[1]
    chunks = samples // length
    nb, hb = samples // W, length // W
    wide = -(-channels // W) * W
    rows_p = -(-channels // 32) * 32
    per_block = W // B
    every = n_atom * atoms
    depth = (length + B - 1) // W + 1
    span = (GROUP + depth - 1) * atoms
    width = max(wide, length)
    chips = n_tm // 2
    factor = 1.0 / math.sqrt(samples * n_tm)
    dma = pltpu.SemaphoreType.DMA
    vmem = pl.BlockSpec(memory_space=pltpu.VMEM)
    return pl.pallas_call(
        functools.partial(kernel, n_atom, n_tm, factor),
        out_shape=(
            pltpu.VMEM((atoms, channels), F32),
            pltpu.VMEM((atoms, length), F32),
        ),
        in_specs=[vmem] * 5,
        out_specs=(vmem, vmem),
        scratch_shapes=[
            pltpu.VMEM((atoms, length), BF16),
            pltpu.VMEM((atoms, length), BF16),
            pltpu.VMEM(((hb + nb) * atoms, W), F32),
            pltpu.VMEM((GROUP * W, W), F32),
            pltpu.VMEM((hb * atoms, W), F32),
            pltpu.VMEM((atoms // 2, (hb + 1) * W, 2 * W), BF16),
            pltpu.VMEM((nb * atoms, W), F32),
            pltpu.VMEM((chunks, every, length), BF16),
            pltpu.VMEM((every, channels), BF16),
            pltpu.VMEM((every, wide), F32),
            pltpu.VMEM((rows_p, every), BF16),
            pltpu.VMEM((atoms, rows_p), BF16),
            pltpu.VMEM((chunks, rows_p, length), BF16),
            pltpu.VMEM((per_block, span, W), F32),
            pltpu.VMEM((B * atoms, W), F32),
            pltpu.VMEM((8 * hb * atoms, W), F32),
            pltpu.VMEM((2, atoms, width), F32),
            pltpu.VMEM((2, atoms // 2, width), F32),
            pltpu.VMEM((2, chips, atoms // 2, width), F32),
            pltpu.VMEM((2, atoms, width), F32),
            dma((2,)),
            dma((n_atom - 1,)),
            dma((n_atom - 1,)),
            dma((n_atom - 1, chunks)),
            dma((n_atom - 1, chunks)),
            dma((2,)),
            dma((2,)),
            dma((2, chips - 1)),
            dma((2, chips - 1)),
            dma((2,)),
            dma((2,)),
        ],
        compiler_params=pltpu.CompilerParams(collective_id=0, has_side_effects=True),
    )(signal, spatial, temporal, values, mask.T)


def solution(mesh):
    in_specs = (P(None, "tm"), P("atom", None), P("atom", None), P("atom", "tm"), P("atom", "tm"))
    out_specs = (P("atom", None), P("atom", None))
    body = functools.partial(local, mesh.shape["atom"], mesh.shape["tm"])
    return jax.shard_map(body, mesh=mesh, in_specs=in_specs, out_specs=out_specs, check_vma=False)
```

time: 31.3 us -> 53.1 us (1.70)
  Pallas kernels: 29.3 us -> 51.1 us
    pallas_call x1, Pallas kernels: 29.3 us -> 51.1 us  [local(): pl.pallas_call(functools.partial(kernel, n_atom, n_tm, factor), out_shape...]
where the time goes in v1:
time: 53.1 us; the launch traced here: 53 us
  Pallas kernels  51.1 us (96%)
  local copies, waits for them, and re-layouts  1.27 us (2%)
  between operations  0.64 us (1%)
    pallas_call x1, Pallas kernels, local(): pl.pallas_call(functools.partial(kernel, n_atom, n_tm, factor), out_shape...  51.1 us
    unnamed x2, local copies, waits for them, and re-layouts  1.27 us

profile of v1, /device:TPU:0, one launch (start us, length us, event | category | flops | bytes accessed | tf_op | source)
XLA Modules:
  0.0 53.0 jit_solution(16048991606920750256)
XLA Ops:
  0.6 51.1 %shard_map.68 = (f32[64,306]{1,0:T(8,128)S(1)}, f32[64,256]{1,0:T(8,128)S(1)}) custom-call(bf16[306,1024]{1,0:T(8,128)(2,1)} %signal_ref.1, bf16[64,306]{1,0:T(8,128)(2,1)} %spatial_ref.1, bf16[64,256]{1,0:T(8,128)(2,1)} %temporal_ref.1, bf16[64,1024]{1,0:T(8,128)(2,1)} %values_ref.1, s32[4,64]{1,0:T(4,128)} %bitcast.1), custom_call_target="tpu_custom_call" | custom-call | tf_op jit(solution)/shard_map/pallas_call | solution.py:345
  51.7 0.6 %copy.9 = f32[64,306]{1,0:T(8,128)} copy(f32[64,306]{1,0:T(8,128)S(1)} %get-tuple-element.2) | data formatting | bytes 156672
  52.4 0.6 %copy.10 = f32[64,256]{1,0:T(8,128)} copy(f32[64,256]{1,0:T(8,128)S(1)} %get-tuple-element.3) | data formatting | bytes 131072

commit v2 on v1

--- a/solution.py
+++ b/solution.py
@@ -37,6 +37,7 @@
     per = chunk // W
     rows_p = st.shape[0]
     wide = sp32.shape[1]
+    span = pj.shape[1] // atoms
     chips = n_tm // 2
     me_a = lax.axis_index("atom")
     me_t = lax.axis_index("tm")
@@ -54,6 +55,20 @@
     for peer in t_peers:
         pl.semaphore_signal(barrier, inc=1, device_id={"tm": peer}, device_id_type=MESH)
 
+    groups = atoms // 8
+
+    def put(ref, count, b, value):
+        for g in range(groups):
+            ref[(g * count + b) * 8 : (g * count + b + 1) * 8, :] = value[8 * g : 8 * g + 8]
+
+    def natural(ref, count, b):
+        return jnp.concatenate(
+            [ref[(g * count + b) * 8 : (g * count + b + 1) * 8, :] for g in range(groups)], axis=0
+        )
+
+    def series(ref, count, g, i, first, size):
+        return ref[pl.ds((g * count + first) * 8 + i, size, stride=8), :]
+
     mask = mask_ref[...].astype(F32).T
     codes = [
         values_ref[:, j * block : (j + 1) * block].astype(F32) * mask[:, j : j + 1]
@@ -61,9 +76,10 @@
     ]
     codes = jnp.concatenate(codes, axis=1)
     tail[...] = codes[:, samples - length :].astype(BF16)
-    cx[: hb * atoms, :] = jnp.zeros((hb * atoms, W), F32)
+    for b in range(hb):
+        put(cx, hb + nb, b, jnp.zeros((atoms, W), F32))
     for b in range(nb):
-        cx[(hb + b) * atoms : (hb + b + 1) * atoms, :] = codes[:, b * W : (b + 1) * W]
+        put(cx, hb + nb, hb + b, codes[:, b * W : (b + 1) * W])
     for d in range(hb):
         wt[d * atoms : (d + 1) * atoms, :] = temporal_ref[:, d * W : (d + 1) * W].astype(F32)
 
@@ -71,11 +87,10 @@
     col = lax.broadcasted_iota(jnp.int32, (W, W), 1)
     ahead = col >= row
 
-    def toeplitz(k):
+    def toeplitz(rows, i):
         circ = [
             pltpu.roll(
-                jnp.broadcast_to(wt[pl.ds(d * atoms + k, 1), :], (W, W)),
-                0, 1, stride=1, stride_axis=0,
+                jnp.broadcast_to(rows[d][i : i + 1], (W, W)), 0, 1, stride=1, stride_axis=0
             )
             for d in range(hb)
         ]
@@ -87,30 +102,33 @@
             parts.append(jnp.where(ahead, near, far))
         return jnp.concatenate(parts, axis=0)
 
-    def windows(k):
+    def windows(g, i):
         return jnp.concatenate(
-            [cx[pl.ds(j * atoms + k, nb, stride=atoms), :] for j in range(hb + 1)], axis=1
-        )
-
-    def apply(p, taps):
-        k = 2 * p
-        lhs = jnp.concatenate([windows(k), windows(k + 1)], axis=0).astype(BF16)
+            [series(cx, hb + nb, g, i, j, nb) for j in range(hb + 1)], axis=1
+        )
+
+    def apply(g, i, taps):
+        lhs = jnp.concatenate([windows(g, i), windows(g, i + 1)], axis=0).astype(BF16)
         out = jnp.dot(lhs, taps, preferred_element_type=F32)
-        cf[pl.ds(k, nb, stride=atoms), :] = out[:nb, :W]
-        cf[pl.ds(k + 1, nb, stride=atoms), :] = out[nb:, W:]
-
-    def first(p, carry):
-        k = 2 * p
-        taps = jnp.concatenate([toeplitz(k), toeplitz(k + 1)], axis=1).astype(BF16)
-        tbuf[p] = taps
-        apply(p, taps)
+        cf[pl.ds(g * nb * 8 + i, nb, stride=8), :] = out[:nb, :W]
+        cf[pl.ds(g * nb * 8 + i + 1, nb, stride=8), :] = out[nb:, W:]
+
+    def first(g, carry):
+        rows = [
+            wt[pl.ds(pl.multiple_of(d * atoms + 8 * g, 8), 8), :] for d in range(hb)
+        ]
+        for i in range(0, 8, 2):
+            taps = jnp.concatenate([toeplitz(rows, i), toeplitz(rows, i + 1)], axis=1).astype(BF16)
+            tbuf[g * 4 + i // 2] = taps
+            apply(g, i, taps)
         return carry
 
-    def again(p, carry):
-        apply(p, tbuf[p])
+    def again(g, carry):
+        for i in range(0, 8, 2):
+            apply(g, i, tbuf[g * 4 + i // 2])
         return carry
 
-    lax.fori_loop(0, atoms // 2, first, 0)
+    lax.fori_loop(0, groups, first, 0)
 
     pl.semaphore_wait(barrier, n_atom - 1 + n_tm - 1)
 
@@ -129,7 +147,7 @@
     def send(c):
         for b in range(per):
             at = c * per + b
-            cbuf[c, mine, b * W : (b + 1) * W] = cf[at * atoms : (at + 1) * atoms, :].astype(BF16)
+            cbuf[c, mine, b * W : (b + 1) * W] = natural(cf, nb, at).astype(BF16)
         for d, peer in enumerate(a_peers):
             copy = pltpu.make_async_remote_copy(
                 src_ref=cbuf.at[c, mine], dst_ref=cbuf.at[c, mine],
@@ -150,8 +168,18 @@
     for c in range(1, chunks):
         send(c)
 
-    xt[length : length + samples, :atoms] = codes.T
-    xt[length + samples :, :] = jnp.zeros((xt.shape[0] - length - samples, W), F32)
+    def lay_time(b, value):
+        turned = value.T
+        for u in range(W // 8):
+            at = (u * GROUP + b) * 8
+            xt[at : at + 8, :atoms] = turned[8 * u : 8 * u + 8]
+
+    for b in range(nb):
+        lay_time(hb + b, codes[:, b * W : (b + 1) * W])
+    for u in range(W // 8):
+        xt[(u * GROUP + hb + nb) * 8 : (u + 1) * GROUP * 8, :] = jnp.zeros(
+            ((GROUP - hb - nb) * 8, W), F32
+        )
     pj[...] = jnp.zeros(pj.shape, F32)
     resb[:, channels // 16 * 16 :, :] = jnp.zeros(
         (chunks, rows_p - channels // 16 * 16, chunk), BF16
@@ -168,22 +196,29 @@
 
     before = halo[...].astype(F32)
     for b in range(hb):
-        cx[b * atoms : (b + 1) * atoms, :] = before[:, b * W : (b + 1) * W]
-    lax.fori_loop(0, atoms // 2, again, 0)
+        put(cx, hb + nb, b, before[:, b * W : (b + 1) * W])
+    lax.fori_loop(0, groups, again, 0)
     send(0)
-    xt[:length, :atoms] = before.T
+    for b in range(hb):
+        lay_time(b, before[:, b * W : (b + 1) * W])
 
     per_block = W // B
 
-    def lay(i, carry):
-        s = B - 1 - i
-        picked = jnp.concatenate(
-            [xt[pl.ds(B * r + s, GROUP, stride=W), :] for r in range(per_block)], axis=0
-        )
-        lt[pl.ds(pl.multiple_of(i * atoms, atoms), atoms), : per_block * GROUP] = picked.T[:atoms]
+    def lay(n, carry):
+        for i in range(8):
+            picked = jnp.concatenate(
+                [
+                    xt[pl.ds((B // 8 * r + B // 8 - 1 - n) * GROUP * 8 + 7 - i, GROUP, stride=8), :]
+                    for r in range(per_block)
+                ],
+                axis=0,
+            ).T
+            for g in range(groups):
+                at = pl.multiple_of((g * B + 8 * n + i) * 8, 8)
+                lt[pl.ds(at, 8), : per_block * GROUP] = picked[8 * g : 8 * g + 8]
         return carry
 
-    lax.fori_loop(0, B, lay, 0)
+    lax.fori_loop(0, B // 8, lay, 0)
 
     sbuf[mine, :] = spatial_ref[...]
     for copy in s_copies:
@@ -204,7 +239,7 @@
         projected = projected.astype(BF16).astype(F32)
         for b in range(per):
             at = hb + c * per + b
-            pj[0, at * atoms : (at + 1) * atoms, :] = projected[:, b * W : (b + 1) * W]
+            put(pj.at[0], span, at, projected[:, b * W : (b + 1) * W])
         grad = lax.dot_general(
             cbuf[c, mine, :], residual, (((1,), (1,)), ((), ())), preferred_element_type=F32
         )
@@ -265,42 +300,43 @@
     lane = lax.broadcasted_iota(jnp.int32, (atoms, W), 1)
     for r in range(1, per_block):
         turned = [
-            pltpu.roll(pj[0, i * atoms : (i + 1) * atoms, :], W - B * r, 1)
+            pltpu.roll(natural(pj.at[0], span, i), W - B * r, 1)
             for i in range(hb, hb + nb)
         ]
         turned = [jnp.zeros((atoms, W), F32)] + turned + [jnp.zeros((atoms, W), F32)]
         for n in range(nb + 1):
-            i = hb - 1 + n
-            pj[r, i * atoms : (i + 1) * atoms, :] = jnp.where(
-                lane < W - B * r, turned[n], turned[n + 1]
+            put(
+                pj.at[r], span, hb - 1 + n,
+                jnp.where(lane < W - B * r, turned[n], turned[n + 1]),
             )
 
     spread_sp = spread(0, sp_lanes, swap_sp)
 
     depth = (length + B - 1) // W + 1
 
-    def correlate(k, carry):
-        lhs = lt[pl.ds(k, B, stride=atoms), :][:, : per_block * GROUP].astype(BF16)
-        rhs = jnp.concatenate(
-            [
-                jnp.concatenate(
-                    [pj[r, pl.ds(j * atoms + k, GROUP, stride=atoms), :] for r in range(per_block)],
-                    axis=0,
-                )
-                for j in range(depth)
-            ],
-            axis=1,
-        ).astype(BF16)
-        prod = jnp.dot(lhs, rhs, preferred_element_type=F32)
-        prod = pltpu.roll(prod, depth * W - (B - 1), 1, stride=1, stride_axis=0)[:, :length]
-        acc = prod[:8]
-        for i in range(1, B // 8):
-            acc = acc + prod[8 * i : 8 * i + 8]
-        for d in range(hb):
-            gt[pl.ds(pl.multiple_of(8 * (d * atoms + k), 8), 8), :] = acc[:, d * W : (d + 1) * W]
+    def correlate(g, carry):
+        for i in range(8):
+            lhs = series(lt, B, g, i, 0, B)[:, : per_block * GROUP].astype(BF16)
+            rhs = jnp.concatenate(
+                [
+                    jnp.concatenate(
+                        [series(pj.at[r], span, g, i, j, GROUP) for r in range(per_block)], axis=0
+                    )
+                    for j in range(depth)
+                ],
+                axis=1,
+            ).astype(BF16)
+            prod = jnp.dot(lhs, rhs, preferred_element_type=F32)
+            prod = pltpu.roll(prod, depth * W - (B - 1), 1, stride=1, stride_axis=0)[:, :length]
+            acc = prod[:8]
+            for q in range(1, B // 8):
+                acc = acc + prod[8 * q : 8 * q + 8]
+            for d in range(hb):
+                at = pl.multiple_of((d * groups + g) * 64 + 8 * i, 8)
+                gt[pl.ds(at, 8), :] = acc[:, d * W : (d + 1) * W]
         return carry
 
-    lax.fori_loop(0, atoms, correlate, 0)
+    lax.fori_loop(0, groups, correlate, 0)
     for d in range(hb):
         gtm = gt[pl.ds(8 * d * atoms, atoms, stride=8), :]
         for i in range(1, 8):

time: 53.1 us -> 31.2 us (0.59)
  Pallas kernels: 51.1 us -> 29.2 us
    pallas_call x1, Pallas kernels: 51.1 us -> 29.2 us  [local(): pl.pallas_call(functools.partial(kernel, n_atom, n_tm, factor), out_shape...]
where the time goes in v2:
time: 31.2 us; the launch traced here: 31.1 us
  Pallas kernels  29.2 us (94%)
  local copies, waits for them, and re-layouts  1.27 us (4%)
  between operations  0.64 us (2%)
    pallas_call x1, Pallas kernels, local(): pl.pallas_call(functools.partial(kernel, n_atom, n_tm, factor), out_shape...  29.2 us
    unnamed x2, local copies, waits for them, and re-layouts  1.27 us

profile of v2, /device:TPU:0, one launch (start us, length us, event | category | flops | bytes accessed | tf_op | source)
XLA Modules:
  0.0 31.1 jit_solution(16643086728870034523)
XLA Ops:
  0.6 29.2 %shard_map.68 = (f32[64,306]{1,0:T(8,128)S(1)}, f32[64,256]{1,0:T(8,128)S(1)}) custom-call(bf16[306,1024]{1,0:T(8,128)(2,1)} %signal_ref.1, bf16[64,306]{1,0:T(8,128)(2,1)} %spatial_ref.1, bf16[64,256]{1,0:T(8,128)(2,1)} %temporal_ref.1, bf16[64,1024]{1,0:T(8,128)(2,1)} %values_ref.1, s32[4,64]{1,0:T(4,128)} %bitcast.1), custom_call_target="tpu_custom_call" | custom-call | tf_op jit(solution)/shard_map/pallas_call | solution.py:381
  29.8 0.6 %copy.9 = f32[64,306]{1,0:T(8,128)} copy(f32[64,306]{1,0:T(8,128)S(1)} %get-tuple-element.2) | data formatting | bytes 156672
  30.5 0.6 %copy.10 = f32[64,256]{1,0:T(8,128)} copy(f32[64,256]{1,0:T(8,128)S(1)} %get-tuple-element.3) | data formatting | bytes 131072

commit v3 on v2

--- a/solution.py
+++ b/solution.py
@@ -14,6 +14,8 @@
 MESH = pl.DeviceIdType.MESH
 F32 = jnp.float32
 BF16 = jnp.bfloat16
+STEPS = 32767.0
+TINY = 2.0**-112
 
 
 def kernel(
@@ -21,7 +23,7 @@
     signal_ref, spatial_ref, temporal_ref, values_ref, mask_ref,
     out_sp_ref, out_tm_ref,
     tail, halo, cx, xt, wt, tbuf, cf, cbuf, sbuf, sp32, st, own_w, resb, pj, lt, gt,
-    part, recv1, half, total,
+    part, recv1, half, scale, total,
     halo_sems, s_send, s_recv, c_send, c_recv,
     p_send, p_recv, z_send, z_recv, f_send, f_recv,
 ):
@@ -263,24 +265,31 @@
 
     def spread(i, lanes, copy):
         copy.wait_recv()
-        half[i, me_z, :, lanes] = part[i, low, lanes] + recv1[i, :, lanes]
+        value = part[i, low, lanes] + recv1[i, :, lanes]
+        top = jnp.max(jnp.abs(value), axis=0, keepdims=True)
+        up = jnp.where(top > TINY, STEPS / jnp.maximum(top, TINY), 0.0)
+        shift = jnp.where(value < 0, -0.5, 0.5)
+        half[i, me_z, :, lanes] = (value * up + shift).astype(jnp.int32).astype(jnp.int16)
+        scale[i, me_z, :, lanes] = top * (1.0 / STEPS)
         copies = []
         for d, peer in enumerate(z_peers):
-            out = pltpu.make_async_remote_copy(
-                src_ref=half.at[i, me_z, :, lanes], dst_ref=half.at[i, me_z, :, lanes],
-                send_sem=z_send.at[i, d], recv_sem=z_recv.at[i, d],
-                device_id={"tm": peer * 2 + core}, device_id_type=MESH,
-            )
-            out.start()
-            copies.append(out)
+            for n, ref in enumerate((half, scale)):
+                out = pltpu.make_async_remote_copy(
+                    src_ref=ref.at[i, me_z, :, lanes], dst_ref=ref.at[i, me_z, :, lanes],
+                    send_sem=z_send.at[i, n, d], recv_sem=z_recv.at[i, n, d],
+                    device_id={"tm": peer * 2 + core}, device_id_type=MESH,
+                )
+                out.start()
+                copies.append(out)
         return copies
 
     def finish(i, lanes, copies):
         for copy in copies:
             copy.wait_recv()
-        acc = half[i, 0, :, lanes]
-        for z in range(1, chips):
-            acc = acc + half[i, z, :, lanes]
+        acc = None
+        for z in range(chips):
+            value = half[i, z, :, lanes].astype(jnp.int32).astype(F32) * scale[i, z, :, lanes]
+            acc = value if acc is None else acc + value
         total[i, low, lanes] = acc * factor
         copy = pltpu.make_async_remote_copy(
             src_ref=total.at[i, low, lanes], dst_ref=total.at[i, low, lanes],
@@ -405,7 +414,8 @@
             pltpu.VMEM((8 * hb * atoms, W), F32),
             pltpu.VMEM((2, atoms, width), F32),
             pltpu.VMEM((2, atoms // 2, width), F32),
-            pltpu.VMEM((2, chips, atoms // 2, width), F32),
+            pltpu.VMEM((2, chips, atoms // 2, width), jnp.int16),
+            pltpu.VMEM((2, chips, 1, width), F32),
             pltpu.VMEM((2, atoms, width), F32),
             dma((2,)),
             dma((n_atom - 1,)),
@@ -414,8 +424,8 @@
             dma((n_atom - 1, chunks)),
             dma((2,)),
             dma((2,)),
-            dma((2, chips - 1)),
-            dma((2, chips - 1)),
+            dma((2, 2, chips - 1)),
+            dma((2, 2, chips - 1)),
             dma((2,)),
             dma((2,)),
         ],

time: 31.2 us -> 30.6 us (0.981)
  Pallas kernels: 29.2 us -> 28.5 us
    pallas_call x1, Pallas kernels: 29.2 us -> 28.5 us  [local(): pl.pallas_call(functools.partial(kernel, n_atom, n_tm, factor), out_shape...]
where the time goes in v3:
time: 30.6 us; the launch traced here: 30.4 us
  Pallas kernels  28.5 us (93%)
  local copies, waits for them, and re-layouts  1.27 us (4%)
  between operations  0.64 us (2%)
    pallas_call x1, Pallas kernels, local(): pl.pallas_call(functools.partial(kernel, n_atom, n_tm, factor), out_shape...  28.5 us
    unnamed x2, local copies, waits for them, and re-layouts  1.27 us

profile of v3, /device:TPU:0, one launch (start us, length us, event | category | flops | bytes accessed | tf_op | source)
XLA Modules:
  0.0 30.4 jit_solution(863166742877504518)
XLA Ops:
  0.6 28.5 %shard_map.68 = (f32[64,306]{1,0:T(8,128)S(1)}, f32[64,256]{1,0:T(8,128)S(1)}) custom-call(bf16[306,1024]{1,0:T(8,128)(2,1)} %signal_ref.1, bf16[64,306]{1,0:T(8,128)(2,1)} %spatial_ref.1, bf16[64,256]{1,0:T(8,128)(2,1)} %temporal_ref.1, bf16[64,1024]{1,0:T(8,128)(2,1)} %values_ref.1, s32[4,64]{1,0:T(4,128)} %bitcast.1), custom_call_target="tpu_custom_call" | custom-call | tf_op jit(solution)/shard_map/pallas_call | solution.py:390
  29.2 0.6 %copy.9 = f32[64,306]{1,0:T(8,128)} copy(f32[64,306]{1,0:T(8,128)S(1)} %get-tuple-element.2) | data formatting | bytes 156672
  29.8 0.6 %copy.10 = f32[64,256]{1,0:T(8,128)} copy(f32[64,256]{1,0:T(8,128)S(1)} %get-tuple-element.3) | data formatting | bytes 131072

commit v4 on v3

--- a/solution.py
+++ b/solution.py
@@ -22,9 +22,9 @@
     n_atom, n_tm, factor,
     signal_ref, spatial_ref, temporal_ref, values_ref, mask_ref,
     out_sp_ref, out_tm_ref,
-    tail, halo, cx, xt, wt, tbuf, cf, cbuf, sbuf, sp32, st, own_w, resb, pj, lt, gt,
+    tail, halo, spill, spilled, cx, xt, wt, cf, cbuf, sbuf, sp32, st, own_w, resb, pj, lt, gt,
     part, recv1, half, scale, total,
-    halo_sems, s_send, s_recv, c_send, c_recv,
+    halo_sems, s_send, s_recv, h_send, h_recv, c_send, c_recv,
     p_send, p_recv, z_send, z_recv, f_send, f_recv,
 ):
     atoms, channels = spatial_ref.shape
@@ -46,9 +46,28 @@
     me_z = me_t // 2
     core = lax.rem(me_t, 2)
     partner = me_z * 2 + 1 - core
-    a_peers = [lax.rem(me_a + d, n_atom) for d in range(1, n_atom)]
+
+    def across(at, count):
+        def flip(d):
+            out = at
+            for bit in range(d.bit_length()):
+                if d >> bit & 1:
+                    step = 1 << bit
+                    out = out + step - 2 * step * lax.rem(at // step, 2)
+            return out
+
+        if count & (count - 1) == 0:
+            return [flip(d) for d in range(count - 1, 0, -1)]
+        return [lax.rem(at + d, count) for d in range(1, count)]
+
+    def sources(at, count):
+        if count & (count - 1) == 0:
+            return across(at, count)
+        return [lax.rem(at + count - d, count) for d in range(1, count)]
+
+    a_peers = across(me_a, n_atom)
     t_peers = [lax.rem(me_t + d, n_tm) for d in range(1, n_tm)]
-    z_peers = [lax.rem(me_z + d, chips) for d in range(1, chips)]
+    z_peers = across(me_z, chips)
     mine = pl.ds(pl.multiple_of(me_a * atoms, atoms), atoms)
 
     barrier = pltpu.get_barrier_semaphore()
@@ -62,6 +81,15 @@
     def put(ref, count, b, value):
         for g in range(groups):
             ref[(g * count + b) * 8 : (g * count + b + 1) * 8, :] = value[8 * g : 8 * g + 8]
+
+    def filtered(b, lo, hi):
+        return jnp.concatenate(
+            [
+                cf[pl.ds((g * (GROUP // 8) + b // 8) * 64 + b % 8, 8, stride=8), :]
+                for g in range(lo, hi)
+            ],
+            axis=0,
+        )
 
     def natural(ref, count, b):
         return jnp.concatenate(
@@ -78,10 +106,11 @@
     ]
     codes = jnp.concatenate(codes, axis=1)
     tail[...] = codes[:, samples - length :].astype(BF16)
-    for b in range(hb):
-        put(cx, hb + nb, b, jnp.zeros((atoms, W), F32))
+    gap = jnp.zeros((atoms, W), F32)
+    for b in list(range(hb)) + list(range(hb + nb, GROUP + hb)):
+        put(cx, GROUP + hb, b, gap)
     for b in range(nb):
-        put(cx, hb + nb, hb + b, codes[:, b * W : (b + 1) * W])
+        put(cx, GROUP + hb, hb + b, codes[:, b * W : (b + 1) * W])
     for d in range(hb):
         wt[d * atoms : (d + 1) * atoms, :] = temporal_ref[:, d * W : (d + 1) * W].astype(F32)
 
@@ -90,13 +119,13 @@
     ahead = col >= row
 
     def toeplitz(rows, i):
-        circ = [
-            pltpu.roll(
-                jnp.broadcast_to(rows[d][i : i + 1], (W, W)), 0, 1, stride=1, stride_axis=0
-            )
-            for d in range(hb)
-        ]
-        zero = jnp.zeros((W, W), F32)
+        circ = []
+        for d in range(hb):
+            base = jnp.broadcast_to(rows[d][i : i + 1], (GROUP, W))
+            base = pltpu.roll(base, 0, 1, stride=1, stride_axis=0).astype(BF16)
+            tiles = [base] + [pltpu.roll(base, GROUP * n, 1) for n in range(1, W // GROUP)]
+            circ.append(jnp.concatenate(tiles, axis=0))
+        zero = jnp.zeros((W, W), BF16)
         parts = []
         for d in range(hb, -1, -1):
             near = circ[d] if d < hb else zero
@@ -106,31 +135,25 @@
 
     def windows(g, i):
         return jnp.concatenate(
-            [series(cx, hb + nb, g, i, j, nb) for j in range(hb + 1)], axis=1
-        )
-
-    def apply(g, i, taps):
-        lhs = jnp.concatenate([windows(g, i), windows(g, i + 1)], axis=0).astype(BF16)
-        out = jnp.dot(lhs, taps, preferred_element_type=F32)
-        cf[pl.ds(g * nb * 8 + i, nb, stride=8), :] = out[:nb, :W]
-        cf[pl.ds(g * nb * 8 + i + 1, nb, stride=8), :] = out[nb:, W:]
+            [series(cx, GROUP + hb, g, i, j, GROUP) for j in range(hb + 1)], axis=1
+        )
 
     def first(g, carry):
         rows = [
             wt[pl.ds(pl.multiple_of(d * atoms + 8 * g, 8), 8), :] for d in range(hb)
         ]
         for i in range(0, 8, 2):
-            taps = jnp.concatenate([toeplitz(rows, i), toeplitz(rows, i + 1)], axis=1).astype(BF16)
-            tbuf[g * 4 + i // 2] = taps
-            apply(g, i, taps)
+            taps = jnp.concatenate([toeplitz(rows, i), toeplitz(rows, i + 1)], axis=1)
+            lhs = jnp.concatenate([windows(g, i), windows(g, i + 1)], axis=0).astype(BF16)
+            out = jnp.dot(lhs, taps, preferred_element_type=F32)
+            for n in range(2):
+                for h in range(GROUP // 8):
+                    at = pl.multiple_of(((g * (GROUP // 8) + h) * 8 + i + n) * 8, 8)
+                    row = n * GROUP + 8 * h
+                    cf[pl.ds(at, 8), :] = out[row : row + 8, n * W : (n + 1) * W]
         return carry
 
-    def again(g, carry):
-        for i in range(0, 8, 2):
-            apply(g, i, tbuf[g * 4 + i // 2])
-        return carry
-
-    lax.fori_loop(0, groups, first, 0)
+    lax.fori_loop(0, groups // 2, first, 0, unroll=4)
 
     pl.semaphore_wait(barrier, n_atom - 1 + n_tm - 1)
 
@@ -140,35 +163,59 @@
         device_id={"tm": right}, device_id_type=MESH,
     )
 
+    spill_copy = pltpu.make_async_remote_copy(
+        src_ref=spill, dst_ref=spilled, send_sem=halo_sems.at[2], recv_sem=halo_sems.at[3],
+        device_id={"tm": right}, device_id_type=MESH,
+    )
     @pl.when(me_t < n_tm - 1)
     def _():
         halo_copy.start()
 
-    c_copies = [[None] * (n_atom - 1) for _ in range(chunks)]
-
-    def send(c):
+    c_copies = [[] for _ in range(chunks)]
+
+    def send(c, lo, hi):
+        rows = pl.ds(pl.multiple_of(me_a * atoms + 8 * lo, 8 * (hi - lo)), 8 * (hi - lo))
         for b in range(per):
-            at = c * per + b
-            cbuf[c, mine, b * W : (b + 1) * W] = natural(cf, nb, at).astype(BF16)
+            value = filtered(c * per + b, lo, hi)
+            if c == 0:
+                value = value + spilled[8 * lo : 8 * hi, b * W : (b + 1) * W]
+            cbuf[c, rows, b * W : (b + 1) * W] = value.astype(BF16)
         for d, peer in enumerate(a_peers):
             copy = pltpu.make_async_remote_copy(
-                src_ref=cbuf.at[c, mine], dst_ref=cbuf.at[c, mine],
-                send_sem=c_send.at[d, c], recv_sem=c_recv.at[d, c],
+                src_ref=cbuf.at[c, rows], dst_ref=cbuf.at[c, rows],
+                send_sem=c_send.at[d, c, 2 * lo // groups], recv_sem=c_recv.at[d, c, 2 * lo // groups],
                 device_id={"atom": peer}, device_id_type=MESH,
             )
             copy.start()
-            c_copies[c][d] = copy
+            c_copies[c].append(copy)
 
     s_copies = []
+    own_half = pl.ds(pl.multiple_of(core * (atoms // 2), atoms // 2), atoms // 2)
+
+    def half_of(peer):
+        at = peer * atoms + core * (atoms // 2)
+        return pl.ds(pl.multiple_of(at, atoms // 2), atoms // 2)
+
     for d, peer in enumerate(a_peers):
         copy = pltpu.make_async_remote_copy(
-            src_ref=spatial_ref, dst_ref=sbuf.at[mine], send_sem=s_send.at[d],
-            recv_sem=s_recv.at[d], device_id={"atom": peer}, device_id_type=MESH,
+            src_ref=spatial_ref.at[own_half], dst_ref=sbuf.at[half_of(me_a)],
+            send_sem=s_send.at[d], recv_sem=s_recv.at[d],
+            device_id={"atom": peer}, device_id_type=MESH,
         )
         copy.start()
         s_copies.append(copy)
     for c in range(1, chunks):
-        send(c)
+        send(c, 0, groups // 2)
+    lax.fori_loop(groups // 2, groups, first, 0, unroll=4)
+    for b in range(hb):
+        spill[:, b * W : (b + 1) * W] = filtered(nb + b, 0, groups)
+
+    @pl.when(me_t < n_tm - 1)
+    def _():
+        spill_copy.start()
+
+    for c in range(1, chunks):
+        send(c, groups // 2, groups)
 
     def lay_time(b, value):
         turned = value.T
@@ -191,6 +238,26 @@
     @pl.when(me_t == 0)
     def _():
         halo[...] = jnp.zeros(halo.shape, halo.dtype)
+        spilled[...] = jnp.zeros(spilled.shape, F32)
+
+    @pl.when(me_t > 0)
+    def _():
+        spill_copy.wait_recv()
+
+    send(0, 0, groups)
+
+    sbuf[mine, :] = spatial_ref[...]
+    passed = []
+    for d, source in enumerate(sources(me_a, n_atom)):
+        s_copies[d].wait_recv()
+        rows = half_of(source)
+        out = pltpu.make_async_remote_copy(
+            src_ref=sbuf.at[rows], dst_ref=sbuf.at[rows],
+            send_sem=h_send.at[d], recv_sem=h_recv.at[d],
+            device_id={"tm": partner}, device_id_type=MESH,
+        )
+        out.start()
+        passed.append(out)
 
     @pl.when(me_t > 0)
     def _():
@@ -198,32 +265,30 @@
 
     before = halo[...].astype(F32)
     for b in range(hb):
-        put(cx, hb + nb, b, before[:, b * W : (b + 1) * W])
-    lax.fori_loop(0, groups, again, 0)
-    send(0)
-    for b in range(hb):
         lay_time(b, before[:, b * W : (b + 1) * W])
 
     per_block = W // B
+    deep = per_block * GROUP
+    slots = W // deep
+    place = lax.rem(lax.broadcasted_iota(jnp.int32, (8, W), 0), slots) == (
+        lax.broadcasted_iota(jnp.int32, (8, W), 1) // deep
+    )
 
     def lay(n, carry):
         for i in range(8):
-            picked = jnp.concatenate(
-                [
-                    xt[pl.ds((B // 8 * r + B // 8 - 1 - n) * GROUP * 8 + 7 - i, GROUP, stride=8), :]
-                    for r in range(per_block)
-                ],
-                axis=0,
-            ).T
+            picked = [
+                xt[pl.ds((B // 8 * r + B // 8 - 1 - n) * GROUP * 8 + 7 - i, GROUP, stride=8), :]
+                for r in range(per_block)
+            ]
+            picked = jnp.concatenate(picked * (W // deep), axis=0).T
             for g in range(groups):
                 at = pl.multiple_of((g * B + 8 * n + i) * 8, 8)
-                lt[pl.ds(at, 8), : per_block * GROUP] = picked[8 * g : 8 * g + 8]
+                lt[pl.ds(at, 8), :] = jnp.where(place, picked[8 * g : 8 * g + 8], 0.0)
         return carry
 
     lax.fori_loop(0, B // 8, lay, 0)
 
-    sbuf[mine, :] = spatial_ref[...]
-    for copy in s_copies:
+    for copy in passed:
         copy.wait_recv()
     sp32[:, :channels] = sbuf[...].astype(F32)
     st[...] = sp32[...].T[:rows_p].astype(BF16)
@@ -319,39 +384,58 @@
                 jnp.where(lane < W - B * r, turned[n], turned[n + 1]),
             )
 
+    depth = (length + B - 1) // W + 1
+
+    def correlate(g, carry):
+        for first_atom in range(0, 8, 2 * slots):
+            some = range(first_atom, first_atom + 2 * slots)
+            lhs = []
+            rhs = []
+            for i in some:
+                left = series(lt, B, g, i, 0, B).astype(BF16)
+                none = jnp.zeros((B, W), BF16)
+                pair = [left, none] if i - first_atom < slots else [none, left]
+                lhs.append(jnp.concatenate(pair, axis=1))
+                for r in range(per_block):
+                    rhs.append(
+                        jnp.concatenate(
+                            [series(pj.at[r], span, g, i, j, GROUP) for j in range(depth)], axis=1
+                        )
+                    )
+            prods = jnp.dot(
+                jnp.concatenate(lhs, axis=0),
+                jnp.concatenate(rhs, axis=0).astype(BF16),
+                preferred_element_type=F32,
+            )
+            for n, i in enumerate(some):
+                prod = prods[n * B : (n + 1) * B]
+                prod = pltpu.roll(prod, depth * W - (B - 1), 1, stride=1, stride_axis=0)
+                acc = prod[:8, :length]
+                for q in range(1, B // 8):
+                    acc = acc + prod[8 * q : 8 * q + 8, :length]
+                for d in range(hb):
+                    at = pl.multiple_of((d * groups + g) * 64 + 8 * i, 8)
+                    gt[pl.ds(at, 8), :] = acc[:, d * W : (d + 1) * W]
+        return carry
+
+    def lags(mine_first, rows):
+        for d in range(hb):
+            at = 8 * (d * atoms + mine_first)
+            total_d = gt[pl.ds(at, atoms // 2, stride=8), :]
+            for i in range(1, 8):
+                total_d = total_d + gt[pl.ds(at + i, atoms // 2, stride=8), :]
+            part[1, rows, d * W : (d + 1) * W] = total_d
+
+    def correlate_from(start, count):
+        lax.fori_loop(0, count, lambda n, carry: correlate(start + n, carry), 0, unroll=count)
+
+    correlate_from((1 - core) * (groups // 2), groups // 2)
+    lags((1 - core) * (atoms // 2), other)
+    swap_tm = swap(1, tm_lanes)
+    correlate_from(core * (groups // 2), groups // 4)
     spread_sp = spread(0, sp_lanes, swap_sp)
-
-    depth = (length + B - 1) // W + 1
-
-    def correlate(g, carry):
-        for i in range(8):
-            lhs = series(lt, B, g, i, 0, B)[:, : per_block * GROUP].astype(BF16)
-            rhs = jnp.concatenate(
-                [
-                    jnp.concatenate(
-                        [series(pj.at[r], span, g, i, j, GROUP) for r in range(per_block)], axis=0
-                    )
-                    for j in range(depth)
-                ],
-                axis=1,
-            ).astype(BF16)
-            prod = jnp.dot(lhs, rhs, preferred_element_type=F32)
-            prod = pltpu.roll(prod, depth * W - (B - 1), 1, stride=1, stride_axis=0)[:, :length]
-            acc = prod[:8]
-            for q in range(1, B // 8):
-                acc = acc + prod[8 * q : 8 * q + 8]
-            for d in range(hb):
-                at = pl.multiple_of((d * groups + g) * 64 + 8 * i, 8)
-                gt[pl.ds(at, 8), :] = acc[:, d * W : (d + 1) * W]
-        return carry
-
-    lax.fori_loop(0, groups, correlate, 0)
-    for d in range(hb):
-        gtm = gt[pl.ds(8 * d * atoms, atoms, stride=8), :]
-        for i in range(1, 8):
-            gtm = gtm + gt[pl.ds(8 * d * atoms + i, atoms, stride=8), :]
-        part[1, :, d * W : (d + 1) * W] = gtm
-    swap_tm = swap(1, tm_lanes)
+    correlate_from(core * (groups // 2) + groups // 4, groups // 4)
+    lags(core * (atoms // 2), low)
     spread_tm = spread(1, tm_lanes, swap_tm)
     last_sp = finish(0, sp_lanes, spread_sp)
     last_tm = finish(1, tm_lanes, spread_tm)
@@ -363,8 +447,9 @@
     @pl.when(me_t < n_tm - 1)
     def _():
         halo_copy.wait_send()
-
-    for copy in s_copies + [copy for line in c_copies for copy in line]:
+        spill_copy.wait_send()
+
+    for copy in s_copies + passed + [copy for line in c_copies for copy in line]:
         copy.wait_send()
     for copy in [swap_sp, swap_tm, last_sp, last_tm] + spread_sp + spread_tm:
         copy.wait_send()
@@ -379,6 +464,11 @@
     wide = -(-channels // W) * W
     rows_p = -(-channels // 32) * 32
     per_block = W // B
+    deep = per_block * GROUP
+    slots = W // deep
+    place = lax.rem(lax.broadcasted_iota(jnp.int32, (8, W), 0), slots) == (
+        lax.broadcasted_iota(jnp.int32, (8, W), 1) // deep
+    )
     every = n_atom * atoms
     depth = (length + B - 1) // W + 1
     span = (GROUP + depth - 1) * atoms
@@ -398,11 +488,12 @@
         scratch_shapes=[
             pltpu.VMEM((atoms, length), BF16),
             pltpu.VMEM((atoms, length), BF16),
-            pltpu.VMEM(((hb + nb) * atoms, W), F32),
+            pltpu.VMEM((atoms, length), F32),
+            pltpu.VMEM((atoms, length), F32),
+            pltpu.VMEM(((GROUP + hb) * atoms, W), F32),
             pltpu.VMEM((GROUP * W, W), F32),
             pltpu.VMEM((hb * atoms, W), F32),
-            pltpu.VMEM((atoms // 2, (hb + 1) * W, 2 * W), BF16),
-            pltpu.VMEM((nb * atoms, W), F32),
+            pltpu.VMEM((GROUP * atoms, W), F32),
             pltpu.VMEM((chunks, every, length), BF16),
             pltpu.VMEM((every, channels), BF16),
             pltpu.VMEM((every, wide), F32),
@@ -417,11 +508,13 @@
             pltpu.VMEM((2, chips, atoms // 2, width), jnp.int16),
             pltpu.VMEM((2, chips, 1, width), F32),
             pltpu.VMEM((2, atoms, width), F32),
-            dma((2,)),
+            dma((4,)),
             dma((n_atom - 1,)),
             dma((n_atom - 1,)),
-            dma((n_atom - 1, chunks)),
-            dma((n_atom - 1, chunks)),
+            dma((n_atom - 1,)),
+            dma((n_atom - 1,)),
+            dma((n_atom - 1, chunks, 2)),
+            dma((n_atom - 1, chunks, 2)),
             dma((2,)),
             dma((2,)),
             dma((2, 2, chips - 1)),

time: 30.6 us -> 26.9 us (0.88)
  Pallas kernels: 28.5 us -> 24.9 us
    pallas_call x1, Pallas kernels: 28.5 us -> 24.9 us  [local(): pl.pallas_call(functools.partial(kernel, n_atom, n_tm, factor), out_shape...]
where the time goes in v4:
time: 26.9 us; the launch traced here: 26.8 us
  Pallas kernels  24.9 us (93%)
  local copies, waits for them, and re-layouts  1.27 us (5%)
  between operations  0.64 us (2%)
    pallas_call x1, Pallas kernels, local(): pl.pallas_call(functools.partial(kernel, n_atom, n_tm, factor), out_shape...  24.9 us
    unnamed x2, local copies, waits for them, and re-layouts  1.27 us

profile of v4, /device:TPU:0, one launch (start us, length us, event | category | flops | bytes accessed | tf_op | source)
XLA Modules:
  0.0 26.8 jit_solution(6291553908499609081)
XLA Ops:
  0.6 24.9 %shard_map.68 = (f32[64,306]{1,0:T(8,128)S(1)}, f32[64,256]{1,0:T(8,128)S(1)}) custom-call(bf16[306,1024]{1,0:T(8,128)(2,1)} %signal_ref.1, bf16[64,306]{1,0:T(8,128)(2,1)} %spatial_ref.1, bf16[64,256]{1,0:T(8,128)(2,1)} %temporal_ref.1, bf16[64,1024]{1,0:T(8,128)(2,1)} %values_ref.1, s32[4,64]{1,0:T(4,128)} %bitcast.1), custom_call_target="tpu_custom_call" | custom-call | tf_op jit(solution)/shard_map/pallas_call | solution.py:480
  25.5 0.6 %copy.9 = f32[64,306]{1,0:T(8,128)} copy(f32[64,306]{1,0:T(8,128)S(1)} %get-tuple-element.2) | data formatting | bytes 156672
  26.1 0.6 %copy.10 = f32[64,256]{1,0:T(8,128)} copy(f32[64,256]{1,0:T(8,128)S(1)} %get-tuple-element.3) | data formatting | bytes 131072

commit v5 on v4

--- a/solution.py
+++ b/solution.py
@@ -11,6 +11,7 @@
 W = 128
 B = 32
 GROUP = 16
+SPLIT = 2
 MESH = pl.DeviceIdType.MESH
 F32 = jnp.float32
 BF16 = jnp.bfloat16
@@ -24,7 +25,7 @@
     out_sp_ref, out_tm_ref,
     tail, halo, spill, spilled, cx, xt, wt, cf, cbuf, sbuf, sp32, st, own_w, resb, pj, lt, gt,
     part, recv1, half, scale, total,
-    halo_sems, s_send, s_recv, h_send, h_recv, c_send, c_recv,
+    heard, halo_sems, s_send, s_recv, h_send, h_recv, c_send, c_recv,
     p_send, p_recv, z_send, z_recv, f_send, f_recv,
 ):
     atoms, channels = spatial_ref.shape
@@ -66,15 +67,42 @@
         return [lax.rem(at + count - d, count) for d in range(1, count)]
 
     a_peers = across(me_a, n_atom)
-    t_peers = [lax.rem(me_t + d, n_tm) for d in range(1, n_tm)]
     z_peers = across(me_z, chips)
     mine = pl.ds(pl.multiple_of(me_a * atoms, atoms), atoms)
 
     barrier = pltpu.get_barrier_semaphore()
     for peer in a_peers:
         pl.semaphore_signal(barrier, inc=1, device_id={"atom": peer}, device_id_type=MESH)
-    for peer in t_peers:
+    line = me_t - 1 + 2 * core
+    beside = [
+        (me_z > 0, me_t - 2),
+        (me_z < chips - 1, me_t + 2),
+        (jnp.logical_and(line >= 0, line < n_tm), line),
+    ]
+
+    def greet(peer):
         pl.semaphore_signal(barrier, inc=1, device_id={"tm": peer}, device_id_type=MESH)
+
+    greet(partner)
+    for there, peer in beside:
+        pl.when(there)(functools.partial(greet, peer))
+
+    def tell(turn):
+        for n, (there, peer) in enumerate(beside[:2]):
+
+            @pl.when(there)
+            def _():
+                pl.semaphore_signal(
+                    heard.at[turn, 1 - n], inc=1, device_id={"tm": peer}, device_id_type=MESH
+                )
+
+    def listen(turn):
+        for n, (there, peer) in enumerate(beside[:2]):
+
+            @pl.when(there)
+            def _():
+                pl.semaphore_wait(heard.at[turn, n], 1)
+
 
     groups = atoms // 8
 
@@ -153,9 +181,14 @@
                     cf[pl.ds(at, 8), :] = out[row : row + 8, n * W : (n + 1) * W]
         return carry
 
-    lax.fori_loop(0, groups // 2, first, 0, unroll=4)
-
-    pl.semaphore_wait(barrier, n_atom - 1 + n_tm - 1)
+    lax.fori_loop(0, SPLIT * groups // 4 // 2 * 2, first, 0, unroll=4)
+
+    present = n_atom
+    for there, _ in beside:
+        present = present + jnp.where(there, 1, 0)
+    pl.semaphore_wait(barrier, present)
+    if chips > 2:
+        tell(0)
 
     right = lax.rem(me_t + 1, n_tm)
     halo_copy = pltpu.make_async_remote_copy(
@@ -163,15 +196,27 @@
         device_id={"tm": right}, device_id_type=MESH,
     )
 
-    spill_copy = pltpu.make_async_remote_copy(
-        src_ref=spill, dst_ref=spilled, send_sem=halo_sems.at[2], recv_sem=halo_sems.at[3],
-        device_id={"tm": right}, device_id_type=MESH,
-    )
-    @pl.when(me_t < n_tm - 1)
-    def _():
-        halo_copy.start()
+    spill_copies = []
+
+    def send_spill(n, lo, hi):
+        rows = slice(8 * lo, 8 * hi)
+        for b in range(hb):
+            spill[rows, b * W : (b + 1) * W] = filtered(nb + b, lo, hi)
+        copy = pltpu.make_async_remote_copy(
+            src_ref=spill.at[rows], dst_ref=spilled.at[rows],
+            send_sem=halo_sems.at[2 + n], recv_sem=halo_sems.at[4 + n],
+            device_id={"tm": right}, device_id_type=MESH,
+        )
+        spill_copies.append(copy)
+
+        @pl.when(me_t < n_tm - 1)
+        def _():
+            copy.start()
 
     c_copies = [[] for _ in range(chunks)]
+    c_waits = [[] for _ in range(chunks)]
+    firsts = {}
+    relays = {1: (2, 1), 2: (1, 2)} if n_atom == 4 and chunks > 2 else {}
 
     def send(c, lo, hi):
         rows = pl.ds(pl.multiple_of(me_a * atoms + 8 * lo, 8 * (hi - lo)), 8 * (hi - lo))
@@ -181,13 +226,42 @@
                 value = value + spilled[8 * lo : 8 * hi, b * W : (b + 1) * W]
             cbuf[c, rows, b * W : (b + 1) * W] = value.astype(BF16)
         for d, peer in enumerate(a_peers):
+            if c in relays and lo == 0 and d == 0:
+                continue
             copy = pltpu.make_async_remote_copy(
                 src_ref=cbuf.at[c, rows], dst_ref=cbuf.at[c, rows],
-                send_sem=c_send.at[d, c, 2 * lo // groups], recv_sem=c_recv.at[d, c, 2 * lo // groups],
+                send_sem=c_send.at[d, c, min(lo, 1)], recv_sem=c_recv.at[d, c, min(lo, 1)],
                 device_id={"atom": peer}, device_id_type=MESH,
             )
             copy.start()
             c_copies[c].append(copy)
+            c_waits[c].append(copy)
+            firsts[c, d, min(lo, 1)] = copy
+
+    def relay(c):
+        source, target = relays[c]
+        copy = firsts[c, source, 0]
+        copy.wait_recv()
+        c_waits[c] = [other_copy for other_copy in c_waits[c] if other_copy is not copy]
+        rows = pl.ds(pl.multiple_of(a_peers[source] * atoms, atoms), 8 * early)
+        copy = pltpu.make_async_remote_copy(
+            src_ref=cbuf.at[c, rows], dst_ref=cbuf.at[c, rows],
+            send_sem=c_send.at[0, c, 0], recv_sem=c_recv.at[0, c, 0],
+            device_id={"atom": a_peers[target]}, device_id_type=MESH,
+        )
+        copy.start()
+        c_copies[c].append(copy)
+        c_waits[c].append(copy)
+
+    early = SPLIT * groups // 4 // 2 * 2
+    send_spill(0, 0, early)
+
+    @pl.when(me_t < n_tm - 1)
+    def _():
+        halo_copy.start()
+
+    for c in relays:
+        send(c, 0, early)
 
     s_copies = []
     own_half = pl.ds(pl.multiple_of(core * (atoms // 2), atoms // 2), atoms // 2)
@@ -205,17 +279,12 @@
         copy.start()
         s_copies.append(copy)
     for c in range(1, chunks):
-        send(c, 0, groups // 2)
-    lax.fori_loop(groups // 2, groups, first, 0, unroll=4)
-    for b in range(hb):
-        spill[:, b * W : (b + 1) * W] = filtered(nb + b, 0, groups)
-
-    @pl.when(me_t < n_tm - 1)
-    def _():
-        spill_copy.start()
-
+        if c not in relays:
+            send(c, 0, early)
+    lax.fori_loop(early, groups, first, 0, unroll=4)
+    send_spill(1, early, groups)
     for c in range(1, chunks):
-        send(c, groups // 2, groups)
+        send(c, early, groups)
 
     def lay_time(b, value):
         turned = value.T
@@ -235,6 +304,9 @@
     )
     sp32[...] = jnp.zeros(sp32.shape, F32)
 
+    for c in relays:
+        relay(c)
+
     @pl.when(me_t == 0)
     def _():
         halo[...] = jnp.zeros(halo.shape, halo.dtype)
@@ -242,9 +314,13 @@
 
     @pl.when(me_t > 0)
     def _():
-        spill_copy.wait_recv()
+        for copy in spill_copies:
+            copy.wait_recv()
 
     send(0, 0, groups)
+    if chips > 3:
+        listen(0)
+        tell(1)
 
     sbuf[mine, :] = spatial_ref[...]
     passed = []
@@ -295,7 +371,7 @@
     own_w[...] = sp32[mine, :rows_p].astype(BF16)
 
     def process(c, gsp):
-        for copy in c_copies[c]:
+        for copy in c_waits[c]:
             copy.wait_recv()
         model = jnp.dot(st[...], cbuf[c], preferred_element_type=F32)
         resb[c, :channels, :] = (
@@ -432,9 +508,13 @@
     correlate_from((1 - core) * (groups // 2), groups // 2)
     lags((1 - core) * (atoms // 2), other)
     swap_tm = swap(1, tm_lanes)
-    correlate_from(core * (groups // 2), groups // 4)
+    for turn in range(1, chips - 3):
+        listen(turn)
+        tell(turn + 1)
+    if chips > 2:
+        listen(chips - 3)
     spread_sp = spread(0, sp_lanes, swap_sp)
-    correlate_from(core * (groups // 2) + groups // 4, groups // 4)
+    correlate_from(core * (groups // 2), groups // 2)
     lags(core * (atoms // 2), low)
     spread_tm = spread(1, tm_lanes, swap_tm)
     last_sp = finish(0, sp_lanes, spread_sp)
@@ -447,7 +527,8 @@
     @pl.when(me_t < n_tm - 1)
     def _():
         halo_copy.wait_send()
-        spill_copy.wait_send()
+        for copy in spill_copies:
+            copy.wait_send()
 
     for copy in s_copies + passed + [copy for line in c_copies for copy in line]:
         copy.wait_send()
@@ -508,7 +589,8 @@
             pltpu.VMEM((2, chips, atoms // 2, width), jnp.int16),
             pltpu.VMEM((2, chips, 1, width), F32),
             pltpu.VMEM((2, atoms, width), F32),
-            dma((4,)),
+            pltpu.SemaphoreType.REGULAR((max(chips - 2, 1), 2)),
+            dma((6,)),
             dma((n_atom - 1,)),
             dma((n_atom - 1,)),
             dma((n_atom - 1,)),
@@ -526,8 +608,32 @@
     )(signal, spatial, temporal, values, mask.T)
 
 
+def settle(a_ref, b_ref, c_ref, d_ref, sems):
+    one = pltpu.make_async_copy(a_ref, c_ref, sems.at[0])
+    two = pltpu.make_async_copy(b_ref, d_ref, sems.at[1])
+    one.start()
+    two.start()
+    one.wait()
+    two.wait()
+
+
+def placed(n_atom, n_tm, *args):
+    first, second = local(n_atom, n_tm, *args)
+    return pl.pallas_call(
+        settle,
+        out_shape=(
+            jax.ShapeDtypeStruct(first.shape, F32),
+            jax.ShapeDtypeStruct(second.shape, F32),
+        ),
+        in_specs=[pl.BlockSpec(memory_space=pltpu.VMEM)] * 2,
+        out_specs=[pl.BlockSpec(memory_space=pltpu.HBM)] * 2,
+        scratch_shapes=[pltpu.SemaphoreType.DMA((2,))],
+        compiler_params=pltpu.CompilerParams(vmem_limit_bytes=1 << 20),
+    )(first, second)
+
+
 def solution(mesh):
     in_specs = (P(None, "tm"), P("atom", None), P("atom", None), P("atom", "tm"), P("atom", "tm"))
     out_specs = (P("atom", None), P("atom", None))
-    body = functools.partial(local, mesh.shape["atom"], mesh.shape["tm"])
+    body = functools.partial(placed, mesh.shape["atom"], mesh.shape["tm"])
     return jax.shard_map(body, mesh=mesh, in_specs=in_specs, out_specs=out_specs, check_vma=False)

time: 26.9 us -> 25.9 us (0.963)
  local copies, waits for them, and re-layouts: 1.27 us -> 0 us
    unnamed x2 -> x0, local copies, waits for them, and re-layouts: 1.27 us -> none
    pallas_call x0 -> x1, Pallas kernels: none -> 0.68 us  [placed(): pl.pallas_call(settle, out_shape=(jax.ShapeDtypeStruct(first.shape, F32),...]
    pallas_call x1, Pallas kernels: 24.9 us -> 24.4 us  [local(): pl.pallas_call(functools.partial(kernel, n_atom, n_tm, factor), out_shape...]
where the time goes in v5:
time: 25.9 us; the launch traced here: 25.7 us
  Pallas kernels  25.1 us (97%)
  between operations  0.64 us (2%)
    pallas_call x1, Pallas kernels, local(): pl.pallas_call(functools.partial(kernel, n_atom, n_tm, factor), out_shape...  24.4 us
    pallas_call x1, Pallas kernels, placed(): pl.pallas_call(settle, out_shape=(jax.ShapeDtypeStruct(first.shape, F32),...  0.68 us

profile of v5, /device:TPU:0, one launch (start us, length us, event | category | flops | bytes accessed | tf_op | source)
XLA Modules:
  0.0 25.7 jit_solution(8670930112355053236)
XLA Ops:
  0.6 24.4 %shard_map.68 = (f32[64,306]{1,0:T(8,128)S(1)}, f32[64,256]{1,0:T(8,128)S(1)}) custom-call(bf16[306,1024]{1,0:T(8,128)(2,1)} %signal_ref.1, bf16[64,306]{1,0:T(8,128)(2,1)} %spatial_ref.1, bf16[64,256]{1,0:T(8,128)(2,1)} %temporal_ref.1, bf16[64,1024]{1,0:T(8,128)(2,1)} %values_ref.1, s32[4,64]{1,0:T(4,128)} %bitcast.1), custom_call_target="tpu_custom_call" | custom-call | tf_op jit(solution)/shard_map/pallas_call | solution.py:561
  25.0 0.7 %shard_map.69 = (f32[64,306]{1,0:T(8,128)}, f32[64,256]{1,0:T(8,128)}) custom-call(f32[64,306]{1,0:T(8,128)S(1)} %get-tuple-element.4.a_ref, f32[64,256]{1,0:T(8,128)S(1)} %get-tuple-element.5.b_ref), custom_call_target="tpu_custom_call" | custom-call | tf_op jit(solution)/shard_map/pallas_call | solution.py:622

commit v6 on v5

--- a/solution.py
+++ b/solution.py
@@ -216,7 +216,10 @@
     c_copies = [[] for _ in range(chunks)]
     c_waits = [[] for _ in range(chunks)]
     firsts = {}
-    relays = {1: (2, 1), 2: (1, 2)} if n_atom == 4 and chunks > 2 else {}
+    relays = {}
+    if n_atom == 4:
+        relays = {c: (2, 1) if c % 2 else (1, 2) for c in range(1, chunks)}
+    order = [chunks - 1] + list(range(1, chunks - 1))
 
     def send(c, lo, hi):
         rows = pl.ds(pl.multiple_of(me_a * atoms + 8 * lo, 8 * (hi - lo)), 8 * (hi - lo))
@@ -283,7 +286,7 @@
             send(c, 0, early)
     lax.fori_loop(early, groups, first, 0, unroll=4)
     send_spill(1, early, groups)
-    for c in range(1, chunks):
+    for c in order:
         send(c, early, groups)
 
     def lay_time(b, value):
@@ -378,18 +381,20 @@
             model[:channels] - signal_ref[:, c * chunk : (c + 1) * chunk].astype(F32)
         ).astype(BF16)
         residual = resb[c]
-        projected = jnp.dot(own_w[...], residual, preferred_element_type=F32)
+        grad = lax.dot_general(
+            cbuf[c, mine, :], residual, (((1,), (1,)), ((), ())), preferred_element_type=F32
+        )
+        return grad if gsp is None else gsp + grad
+
+    def project(c):
+        projected = jnp.dot(own_w[...], resb[c], preferred_element_type=F32)
         projected = projected.astype(BF16).astype(F32)
         for b in range(per):
             at = hb + c * per + b
             put(pj.at[0], span, at, projected[:, b * W : (b + 1) * W])
-        grad = lax.dot_general(
-            cbuf[c, mine, :], residual, (((1,), (1,)), ((), ())), preferred_element_type=F32
-        )
-        return grad if gsp is None else gsp + grad
 
     gsp = None
-    for c in list(range(1, chunks)) + [0]:
+    for c in order + [0]:
         gsp = process(c, gsp)
 
     low = pl.ds(pl.multiple_of(core * (atoms // 2), atoms // 2), atoms // 2)
@@ -446,6 +451,8 @@
     if rows_p < wide:
         part[0, :, rows_p:] = jnp.zeros((atoms, wide - rows_p), F32)
     swap_sp = swap(0, sp_lanes)
+    for c in range(chunks):
+        project(c)
 
     lane = lax.broadcasted_iota(jnp.int32, (atoms, W), 1)
     for r in range(1, per_block):
@@ -505,15 +512,15 @@
     def correlate_from(start, count):
         lax.fori_loop(0, count, lambda n, carry: correlate(start + n, carry), 0, unroll=count)
 
-    correlate_from((1 - core) * (groups // 2), groups // 2)
-    lags((1 - core) * (atoms // 2), other)
-    swap_tm = swap(1, tm_lanes)
     for turn in range(1, chips - 3):
         listen(turn)
         tell(turn + 1)
     if chips > 2:
         listen(chips - 3)
     spread_sp = spread(0, sp_lanes, swap_sp)
+    correlate_from((1 - core) * (groups // 2), groups // 2)
+    lags((1 - core) * (atoms // 2), other)
+    swap_tm = swap(1, tm_lanes)
     correlate_from(core * (groups // 2), groups // 2)
     lags(core * (atoms // 2), low)
     spread_tm = spread(1, tm_lanes, swap_tm)

time: 25.9 us -> 25.4 us (0.981)
  Pallas kernels: 25.1 us -> 24.6 us
    pallas_call x1, Pallas kernels: 24.4 us -> 23.9 us  [local(): pl.pallas_call(functools.partial(kernel, n_atom, n_tm, factor), out_shape...]
where the time goes in v6:
time: 25.4 us; the launch traced here: 25.2 us
  Pallas kernels  24.6 us (97%)
  between operations  0.64 us (3%)
    pallas_call x1, Pallas kernels, local(): pl.pallas_call(functools.partial(kernel, n_atom, n_tm, factor), out_shape...  23.9 us
    pallas_call x1, Pallas kernels, placed(): pl.pallas_call(settle, out_shape=(jax.ShapeDtypeStruct(first.shape, F32),...  0.68 us

profile of v6, /device:TPU:0, one launch (start us, length us, event | category | flops | bytes accessed | tf_op | source)
XLA Modules:
  0.0 25.2 jit_solution(14813258058717465319)
XLA Ops:
  0.6 23.9 %shard_map.68 = (f32[64,306]{1,0:T(8,128)S(1)}, f32[64,256]{1,0:T(8,128)S(1)}) custom-call(bf16[306,1024]{1,0:T(8,128)(2,1)} %signal_ref.1, bf16[64,306]{1,0:T(8,128)(2,1)} %spatial_ref.1, bf16[64,256]{1,0:T(8,128)(2,1)} %temporal_ref.1, bf16[64,1024]{1,0:T(8,128)(2,1)} %values_ref.1, s32[4,64]{1,0:T(4,128)} %bitcast.1), custom_call_target="tpu_custom_call" | custom-call | tf_op jit(solution)/shard_map/pallas_call | solution.py:568
  24.5 0.7 %shard_map.69 = (f32[64,306]{1,0:T(8,128)}, f32[64,256]{1,0:T(8,128)}) custom-call(f32[64,306]{1,0:T(8,128)S(1)} %get-tuple-element.4.a_ref, f32[64,256]{1,0:T(8,128)S(1)} %get-tuple-element.5.b_ref), custom_call_target="tpu_custom_call" | custom-call | tf_op jit(solution)/shard_map/pallas_call | solution.py:629

commit v7 on v6

--- a/solution.py
+++ b/solution.py
@@ -24,7 +24,7 @@
     signal_ref, spatial_ref, temporal_ref, values_ref, mask_ref,
     out_sp_ref, out_tm_ref,
     tail, halo, spill, spilled, cx, xt, wt, cf, cbuf, sbuf, sp32, st, own_w, resb, pj, lt, gt,
-    part, recv1, half, scale, total,
+    part, recv1, half, folded, scale, total,
     heard, halo_sems, s_send, s_recv, h_send, h_recv, c_send, c_recv,
     p_send, p_recv, z_send, z_recv, f_send, f_recv,
 ):
@@ -409,19 +409,33 @@
         copy.start()
         return copy
 
-    def spread(i, lanes, copy):
-        copy.wait_recv()
-        value = part[i, low, lanes] + recv1[i, :, lanes]
+    def encode(value):
         top = jnp.max(jnp.abs(value), axis=0, keepdims=True)
         up = jnp.where(top > TINY, STEPS / jnp.maximum(top, TINY), 0.0)
         shift = jnp.where(value < 0, -0.5, 0.5)
-        half[i, me_z, :, lanes] = (value * up + shift).astype(jnp.int32).astype(jnp.int16)
-        scale[i, me_z, :, lanes] = top * (1.0 / STEPS)
+        return value * up + shift, top * (1.0 / STEPS)
+
+    def spread(i, lanes, copy):
+        copy.wait_recv()
+        value, step = encode(part[i, low, lanes] + recv1[i, :, lanes])
+        scale[i, me_z, :, lanes] = step
+        refs = [half.at[i, me_z, :, lanes], scale.at[i, me_z, :, lanes]]
+        if i == 0 and fold:
+            rest = value[:, wide - W :]
+            rest = jnp.where(
+                low_lane, rest[: atoms // 4], pltpu.roll(rest[atoms // 4 :], W // 2, 1)
+            )
+            folded[me_z] = rest.astype(jnp.int32).astype(jnp.int16)
+            lanes = slice(0, wide - W)
+            refs[0] = half.at[i, me_z, :, lanes]
+            refs.append(folded.at[me_z])
+            value = value[:, : wide - W]
+        half[i, me_z, :, lanes] = value.astype(jnp.int32).astype(jnp.int16)
         copies = []
         for d, peer in enumerate(z_peers):
-            for n, ref in enumerate((half, scale)):
+            for n, ref in enumerate(refs):
                 out = pltpu.make_async_remote_copy(
-                    src_ref=ref.at[i, me_z, :, lanes], dst_ref=ref.at[i, me_z, :, lanes],
+                    src_ref=ref, dst_ref=ref,
                     send_sem=z_send.at[i, n, d], recv_sem=z_recv.at[i, n, d],
                     device_id={"tm": peer * 2 + core}, device_id_type=MESH,
                 )
@@ -434,7 +448,14 @@
             copy.wait_recv()
         acc = None
         for z in range(chips):
-            value = half[i, z, :, lanes].astype(jnp.int32).astype(F32) * scale[i, z, :, lanes]
+            if i == 0 and fold:
+                rest = folded[z].astype(jnp.int32).astype(F32)
+                rest = jnp.concatenate([rest, pltpu.roll(rest, W // 2, 1)], axis=0)
+                value = half[i, z, :, : wide - W].astype(jnp.int32).astype(F32)
+                value = jnp.concatenate([value, rest], axis=1)
+            else:
+                value = half[i, z, :, lanes].astype(jnp.int32).astype(F32)
+            value = value * scale[i, z, :, lanes]
             acc = value if acc is None else acc + value
         total[i, low, lanes] = acc * factor
         copy = pltpu.make_async_remote_copy(
@@ -445,6 +466,8 @@
         copy.start()
         return copy
 
+    fold = wide > W and channels - (wide - W) <= W // 2 and atoms % 64 == 0
+    low_lane = lax.broadcasted_iota(jnp.int32, (atoms // 4, W), 1) < W // 2
     sp_lanes = slice(0, wide)
     tm_lanes = slice(0, length)
     part[0, :, :rows_p] = gsp
@@ -594,6 +617,7 @@
             pltpu.VMEM((2, atoms, width), F32),
             pltpu.VMEM((2, atoms // 2, width), F32),
             pltpu.VMEM((2, chips, atoms // 2, width), jnp.int16),
+            pltpu.VMEM((chips, max(atoms // 4, GROUP), W), jnp.int16),
             pltpu.VMEM((2, chips, 1, width), F32),
             pltpu.VMEM((2, atoms, width), F32),
             pltpu.SemaphoreType.REGULAR((max(chips - 2, 1), 2)),
@@ -606,8 +630,8 @@
             dma((n_atom - 1, chunks, 2)),
             dma((2,)),
             dma((2,)),
-            dma((2, 2, chips - 1)),
-            dma((2, 2, chips - 1)),
+            dma((2, 3, chips - 1)),
+            dma((2, 3, chips - 1)),
             dma((2,)),
             dma((2,)),
         ],

time: 25.4 us -> 25.2 us (level)
  no operation moved by 1% of the time
where the time goes in v7:
time: 25.2 us; the launch traced here: 25.1 us
  Pallas kernels  24.5 us (97%)
  between operations  0.64 us (3%)
    pallas_call x1, Pallas kernels, local(): pl.pallas_call(functools.partial(kernel, n_atom, n_tm, factor), out_shape...  23.8 us
    pallas_call x1, Pallas kernels, placed(): pl.pallas_call(settle, out_shape=(jax.ShapeDtypeStruct(first.shape, F32),...  0.68 us

profile of v7, /device:TPU:0, one launch (start us, length us, event | category | flops | bytes accessed | tf_op | source)
XLA Modules:
  0.0 25.1 jit_solution(16464593843151621464)
XLA Ops:
  0.6 23.8 %shard_map.68 = (f32[64,306]{1,0:T(8,128)S(1)}, f32[64,256]{1,0:T(8,128)S(1)}) custom-call(bf16[306,1024]{1,0:T(8,128)(2,1)} %signal_ref.1, bf16[64,306]{1,0:T(8,128)(2,1)} %spatial_ref.1, bf16[64,256]{1,0:T(8,128)(2,1)} %temporal_ref.1, bf16[64,1024]{1,0:T(8,128)(2,1)} %values_ref.1, s32[4,64]{1,0:T(4,128)} %bitcast.1), custom_call_target="tpu_custom_call" | custom-call | tf_op jit(solution)/shard_map/pallas_call | solution.py:591
  24.4 0.7 %shard_map.69 = (f32[64,306]{1,0:T(8,128)}, f32[64,256]{1,0:T(8,128)}) custom-call(f32[64,306]{1,0:T(8,128)S(1)} %get-tuple-element.4.a_ref, f32[64,256]{1,0:T(8,128)S(1)} %get-tuple-element.5.b_ref), custom_call_target="tpu_custom_call" | custom-call | tf_op jit(solution)/shard_map/pallas_call | solution.py:653

commit v8 on v7

--- a/solution.py
+++ b/solution.py
@@ -406,7 +406,6 @@
             send_sem=p_send.at[i], recv_sem=p_recv.at[i],
             device_id={"tm": partner}, device_id_type=MESH,
         )
-        copy.start()
         return copy
 
     def encode(value):
@@ -474,6 +473,7 @@
     if rows_p < wide:
         part[0, :, rows_p:] = jnp.zeros((atoms, wide - rows_p), F32)
     swap_sp = swap(0, sp_lanes)
+    swap_sp.start()
     for c in range(chunks):
         project(c)
 
@@ -535,15 +535,21 @@
     def correlate_from(start, count):
         lax.fori_loop(0, count, lambda n, carry: correlate(start + n, carry), 0, unroll=count)
 
+    swap_tm = swap(1, tm_lanes)
+
+    def theirs():
+        correlate_from((1 - core) * (groups // 2), groups // 2)
+        lags((1 - core) * (atoms // 2), other)
+        swap_tm.start()
+
+    pl.when(core == 1)(theirs)
     for turn in range(1, chips - 3):
         listen(turn)
         tell(turn + 1)
     if chips > 2:
         listen(chips - 3)
     spread_sp = spread(0, sp_lanes, swap_sp)
-    correlate_from((1 - core) * (groups // 2), groups // 2)
-    lags((1 - core) * (atoms // 2), other)
-    swap_tm = swap(1, tm_lanes)
+    pl.when(core == 0)(theirs)
     correlate_from(core * (groups // 2), groups // 2)
     lags(core * (atoms // 2), low)
     spread_tm = spread(1, tm_lanes, swap_tm)

time: 25.2 us -> 25.1 us (level)
  no operation moved by 1% of the time
where the time goes in v8:
time: 25.1 us; the launch traced here: 25 us
  Pallas kernels  24.3 us (97%)
  between operations  0.64 us (3%)
    pallas_call x1, Pallas kernels, local(): pl.pallas_call(functools.partial(kernel, n_atom, n_tm, factor), out_shape...  23.6 us
    pallas_call x1, Pallas kernels, placed(): pl.pallas_call(settle, out_shape=(jax.ShapeDtypeStruct(first.shape, F32),...  0.68 us

profile of v8, /device:TPU:0, one launch (start us, length us, event | category | flops | bytes accessed | tf_op | source)
XLA Modules:
  0.0 25.0 jit_solution(8199646310079432126)
XLA Ops:
  0.6 23.6 %shard_map.68 = (f32[64,306]{1,0:T(8,128)S(1)}, f32[64,256]{1,0:T(8,128)S(1)}) custom-call(bf16[306,1024]{1,0:T(8,128)(2,1)} %signal_ref.1, bf16[64,306]{1,0:T(8,128)(2,1)} %spatial_ref.1, bf16[64,256]{1,0:T(8,128)(2,1)} %temporal_ref.1, bf16[64,1024]{1,0:T(8,128)(2,1)} %values_ref.1, s32[4,64]{1,0:T(4,128)} %bitcast.1), custom_call_target="tpu_custom_call" | custom-call | tf_op jit(solution)/shard_map/pallas_call | solution.py:597
  24.3 0.7 %shard_map.69 = (f32[64,306]{1,0:T(8,128)}, f32[64,256]{1,0:T(8,128)}) custom-call(f32[64,306]{1,0:T(8,128)S(1)} %get-tuple-element.4.a_ref, f32[64,256]{1,0:T(8,128)S(1)} %get-tuple-element.5.b_ref), custom_call_target="tpu_custom_call" | custom-call | tf_op jit(solution)/shard_map/pallas_call | solution.py:659

commit v9 on v8

--- a/solution.py
+++ b/solution.py
@@ -183,6 +183,11 @@
 
     lax.fori_loop(0, SPLIT * groups // 4 // 2 * 2, first, 0, unroll=4)
 
+    @pl.when(me_a == 0)
+    def _():
+        lax.fori_loop(SPLIT * groups // 4 // 2 * 2, groups, first, 0, unroll=4)
+
+
     present = n_atom
     for there, _ in beside:
         present = present + jnp.where(there, 1, 0)
@@ -219,7 +224,7 @@
     relays = {}
     if n_atom == 4:
         relays = {c: (2, 1) if c % 2 else (1, 2) for c in range(1, chunks)}
-    order = [chunks - 1] + list(range(1, chunks - 1))
+    order = list(range(1, chunks))
 
     def send(c, lo, hi):
         rows = pl.ds(pl.multiple_of(me_a * atoms + 8 * lo, 8 * (hi - lo)), 8 * (hi - lo))
@@ -284,7 +289,10 @@
     for c in range(1, chunks):
         if c not in relays:
             send(c, 0, early)
-    lax.fori_loop(early, groups, first, 0, unroll=4)
+    @pl.when(me_a > 0)
+    def _():
+        lax.fori_loop(early, groups, first, 0, unroll=4)
+
     send_spill(1, early, groups)
     for c in order:
         send(c, early, groups)

time: 25.1 us -> 25.1 us (level)
  no operation moved by 1% of the time
where the time goes in v9:
time: 25.1 us; the launch traced here: 25 us
  Pallas kernels  24.3 us (97%)
  between operations  0.64 us (3%)
    pallas_call x1, Pallas kernels, local(): pl.pallas_call(functools.partial(kernel, n_atom, n_tm, factor), out_shape...  23.6 us
    pallas_call x1, Pallas kernels, placed(): pl.pallas_call(settle, out_shape=(jax.ShapeDtypeStruct(first.shape, F32),...  0.68 us

profile of v9, /device:TPU:0, one launch (start us, length us, event | category | flops | bytes accessed | tf_op | source)
XLA Modules:
  0.0 25.0 jit_solution(9183023258574381394)
XLA Ops:
  0.6 23.6 %shard_map.68 = (f32[64,306]{1,0:T(8,128)S(1)}, f32[64,256]{1,0:T(8,128)S(1)}) custom-call(bf16[306,1024]{1,0:T(8,128)(2,1)} %signal_ref.1, bf16[64,306]{1,0:T(8,128)(2,1)} %spatial_ref.1, bf16[64,256]{1,0:T(8,128)(2,1)} %temporal_ref.1, bf16[64,1024]{1,0:T(8,128)(2,1)} %values_ref.1, s32[4,64]{1,0:T(4,128)} %bitcast.1), custom_call_target="tpu_custom_call" | custom-call | tf_op jit(solution)/shard_map/pallas_call | solution.py:605
  24.3 0.7 %shard_map.69 = (f32[64,306]{1,0:T(8,128)}, f32[64,256]{1,0:T(8,128)}) custom-call(f32[64,306]{1,0:T(8,128)S(1)} %get-tuple-element.4.a_ref, f32[64,256]{1,0:T(8,128)S(1)} %get-tuple-element.5.b_ref), custom_call_target="tpu_custom_call" | custom-call | tf_op jit(solution)/shard_map/pallas_call | solution.py:667
